TPU v7x, 256 devices: a whole 4x4x8 slice. The times are simulated.
256 devices in a mesh: section: 2 (over core), tensor: 2 (over x_lo), dp: 64 (over z, y, x_hi).
Axes of the slice: x: 4 (x_hi: 2, x_lo: 2; x = x_hi * 2 + x_lo), y: 4, z: 8, core: 2. Of those that a mesh axis runs over, the one named last changes fastest.
Arguments:
- exit_hidden: bfloat16 [512, 4, 2048], P('dp', None, ('section', 'tensor')), may hold values from -6 to 6
- exit_depth: int32 [512], P('dp'), may hold values from 0 to 1, as said below
- context_len: int32 [512], P('dp'), may hold values from 48 to 384
- attn_gain: float32 [2, 2048], P('section'), may hold values from 0.1 to 1.9
- w_query: bfloat16 [2, 2048, 2048], P('section', None, 'tensor'), may hold values from -0.125 to 0.125
- w_keyval: bfloat16 [2, 2048, 1024], P('section', None, 'tensor'), may hold values from -0.125 to 0.125
- w_out: bfloat16 [2, 2048, 2048], P('section', 'tensor'), may hold values from -0.125 to 0.125
- kv_cache: bfloat16 [2, 512, 384, 8, 128], P('section', 'dp', None, 'tensor'), may hold values from -400 to 400
- mlp_gain: float32 [2, 2048], P('section'), may hold values from 0.1 to 1.9
- w_gate: bfloat16 [2, 2048, 4096], P('section', 'dp', 'tensor'), may hold values from -0.125 to 0.125
- w_up: bfloat16 [2, 2048, 4096], P('section', 'dp', 'tensor'), may hold values from -0.125 to 0.125
- w_down: bfloat16 [2, 2048, 4096], P('section', 'dp', 'tensor'), may hold values from -0.09375 to 0.09375
Outputs:
- layer_states: bfloat16 [2, 512, 4, 2048], P('section', 'dp', None, 'tensor')
Inputs may be any that keep to these rules, and one draw needn't show every extreme that they name: `exit_depth`: every depth from 0 to 1 is held by some request.
All inputs are finite; a program needn't handle non-finite values.
Results may differ from a plain program's by a relative error of at most 0.019.
Values may be sent and summed in bfloat16 or wider, within the bound.
No kernel may reach another device: no remote copies, remote signals or barrier semaphores. Data moves between devices by JAX's collectives and lax.ppermute only.
A program may use at most 192 MiB of HBM per device.

v0:
```python
import functools
import math

import jax
import jax.numpy as jnp
from jax import lax
from jax.experimental import pallas as pl
from jax.experimental.pallas import tpu as pltpu
from jax.sharding import Mesh, PartitionSpec as P


D = 2048
DRAFT = 4
CTX = 384
ROWS = 8
TOKENS = ROWS * DRAFT
HD = 64
QH = 16
KH = 4
SLOTS = CTX * KH
VMEM_LIMIT = 53000 * 1024
AHEAD = 5
FFS = 256
EPS = 1e-05
THETA = 500000.0
NEGATIVE = -1e30
GROUPS = ((("tensor", "y", "xh"), 16), (("tensor", "y"), 8))
CHIP = ("section", "tensor")
Z = 8


def attend_kernel(
    by_token, lens, me, *refs
):
    pieces, refs = refs[:4], refs[4:]
    gain_h, cos_h, sin_h, wq_h, wkv_h, wo_h, kv_h, *refs = refs
    out, refs = refs[:4], refs[4:]
    kept, half, *refs = refs
    hidden, gain, cosine, sine, wq, wkv, wo, kv, qs, nk, hs, bias, result, sems = refs
    mine = me[0]
    small = []
    small.append(pltpu.make_async_copy(gain_h, gain, sems.at[4]))
    small.append(pltpu.make_async_copy(cos_h, cosine, sems.at[5]))
    small.append(pltpu.make_async_copy(sin_h, sine, sems.at[6]))
    chunks = 8
    step = D // chunks
    copies = []
    for p in range(chunks):
        at = pl.ds(p * step, step)
        copies.append(pltpu.make_async_copy(wq_h.at[at], wq.at[at], sems.at[7 + 2 * p]))
        copies.append(pltpu.make_async_copy(wkv_h.at[at], wkv.at[at], sems.at[8 + 2 * p]))
    base = 7 + 2 * chunks
    kv_copies = [
        pltpu.make_async_copy(kv_h.at[r], kv.at[r], sems.at[base + r]) for r in range(ROWS)
    ]
    wo_copies = [
        pltpu.make_async_copy(
            wo_h.at[pl.ds(p * 256, 256)], wo.at[pl.ds(p * 256, 256)], sems.at[base + ROWS + p]
        )
        for p in range(4)
    ]
    queue = [copies[2 * p : 2 * p + 2] for p in range(chunks)] + [
        kv_copies[2 * p : 2 * p + 2] for p in range(ROWS // 2)
    ]
    queue += [[c] for c in wo_copies]
    for c in small:
        c.start()
    for group in queue[:AHEAD]:
        for c in group:
            c.start()

    def arrived(n):
        for c in queue[n]:
            c.wait()
        if n + AHEAD < len(queue):
            for c in queue[n + AHEAD]:
                c.start()

    row = lax.broadcasted_iota(jnp.int32, (4 * QH, SLOTS), 0)
    place = lax.broadcasted_iota(jnp.int32, (4 * QH, SLOTS), 1)
    bias[...] = jnp.where((place & 3) == (row >> 4), 0.0, NEGATIVE)
    new_row = lax.broadcasted_iota(jnp.int32, (4 * QH, DRAFT * KH), 0)
    new_col = lax.broadcasted_iota(jnp.int32, (4 * QH, DRAFT * KH), 1)
    seen = ((new_col & 3) == (new_row >> 4)) & ((new_col >> 2) <= (new_row & 3))

    for k in range(4):
        other = mine ^ k
        if by_token:
            hidden[other] = pieces[k][...]
        else:
            hidden[:, :, pl.ds(pl.multiple_of(other * 512, 512), 512)] = pieces[k][...]
    for c in small:
        c.wait()
    kept[...] = hidden[mine]
    if by_token:
        half[...] = jnp.where((mine & 1) == 0, hidden[:, :, : D // 2], hidden[:, :, D // 2 :])
    wide = hidden[...].astype(jnp.float32).reshape(TOKENS, D)
    factor = lax.rsqrt(jnp.mean(wide * wide, axis=-1, keepdims=True) + EPS)
    normed = (wide * factor * gain[...]).astype(jnp.bfloat16)
    q = jnp.zeros((TOKENS, QH * HD), jnp.float32)
    new = jnp.zeros((TOKENS, KH * 2 * HD), jnp.float32)
    for p in range(chunks):
        at = pl.ds(p * step, step)
        arrived(p)
        part = normed[:, p * step : (p + 1) * step]
        q = q + jnp.dot(part, wq[at], preferred_element_type=jnp.float32)
        new = new + jnp.dot(part, wkv[at], preferred_element_type=jnp.float32)

    lane = lax.broadcasted_iota(jnp.int32, (TOKENS, 128), 1)
    low = (lane & 63) < 32
    left = lane < HD
    cos_all = cosine[...]
    sin_all = sine[...]

    def turned(block, c, s):
        other = jnp.where(low, pltpu.roll(block, 96, 1), pltpu.roll(block, 32, 1))
        return block * c + other * s

    scale = HD ** (-0.5)
    for m in range(QH // 2):
        block = turned(q[:, m * 128 : (m + 1) * 128], cos_all, sin_all) * scale
        pair = (jnp.where(left, block, 0.0), jnp.where(left, pltpu.roll(block, HD, 1), 0.0))
        for half in range(2):
            for j in range(DRAFT):
                at = ((2 * m + half) * DRAFT + j) * ROWS
                qs[at : at + ROWS, :] = pair[half][j * ROWS : (j + 1) * ROWS, :]
    key_cos = jnp.where(left, cos_all, 1.0)
    key_sin = jnp.where(left, sin_all, 0.0)
    for h in range(KH):
        block = turned(new[:, h * 128 : (h + 1) * 128], key_cos, key_sin)
        for i in range(DRAFT):
            at = (i * KH + h) * ROWS
            nk[at : at + ROWS, :] = block[i * ROWS : (i + 1) * ROWS, :]

    last = (((1,), (1,)), ((), ()))
    for r in range(ROWS):
        fresh = nk[pl.ds(r, DRAFT * KH, stride=ROWS), :].astype(jnp.bfloat16)
        asked = qs[pl.ds(r, 4 * QH, stride=ROWS), :].astype(jnp.bfloat16)
        if r % 2 == 0:
            arrived(chunks + r // 2)
        stored = kv[r]
        scores = lax.dot_general(asked, stored, last, preferred_element_type=jnp.float32)
        scores = jnp.where(place < KH * lens[r], scores, NEGATIVE) + bias[...]
        new_scores = lax.dot_general(asked, fresh, last, preferred_element_type=jnp.float32)
        new_scores = jnp.where(seen, new_scores, NEGATIVE)
        top = jnp.maximum(
            jnp.max(scores, axis=-1, keepdims=True), jnp.max(new_scores, axis=-1, keepdims=True)
        )
        weights = jnp.exp(scores - top)
        new_weights = jnp.exp(new_scores - top)
        total = jnp.sum(weights, axis=-1, keepdims=True) + jnp.sum(
            new_weights, axis=-1, keepdims=True
        )
        mixed = jnp.dot(
            weights.astype(jnp.bfloat16), stored, preferred_element_type=jnp.float32
        ) + jnp.dot(new_weights.astype(jnp.bfloat16), fresh, preferred_element_type=jnp.float32)
        hs[pl.ds(r, 4 * QH, stride=ROWS), :] = mixed / total

    side = lax.broadcasted_iota(jnp.int32, (ROWS, 128), 1) < HD
    rows = []
    for j in range(DRAFT):
        tiles = []
        for m in range(QH // 2):
            first = ((2 * m) * DRAFT + j) * ROWS
            second = ((2 * m + 1) * DRAFT + j) * ROWS
            tiles.append(
                jnp.where(
                    side, pltpu.roll(hs[first : first + ROWS, :], HD, 1), hs[second : second + ROWS, :]
                )
            )
        rows.append(jnp.concatenate(tiles, axis=1))
    heads = jnp.concatenate(rows, axis=0).astype(jnp.bfloat16)
    for p in range(4):
        arrived(chunks + ROWS // 2 + p)
    shares = jnp.dot(heads, wo[...], preferred_element_type=jnp.float32)
    for j in range(DRAFT):
        result[j] = shares[j * ROWS : (j + 1) * ROWS, :].astype(jnp.bfloat16)
    for k in range(4):
        out[k][...] = result[mine ^ k]


def attend(by_token, lens, me, pieces, gain, cosine, sine, wq, wkv, wo, kv):
    hbm = pl.BlockSpec(memory_space=pltpu.HBM)
    vmem = pl.BlockSpec(memory_space=pltpu.VMEM)
    smem = pl.BlockSpec(memory_space=pltpu.SMEM)
    quarter = jax.ShapeDtypeStruct((ROWS, D), jnp.bfloat16)
    return pl.pallas_call(
        functools.partial(attend_kernel, by_token),
        out_shape=[quarter] * 5 + [jax.ShapeDtypeStruct((DRAFT, ROWS, D // 2), jnp.bfloat16)],
        in_specs=[smem] * 2 + [vmem] * 4 + [hbm] * 7,
        out_specs=[vmem] * 6,
        scratch_shapes=[
            pltpu.VMEM((DRAFT, ROWS, D), jnp.bfloat16),
            pltpu.VMEM((1, D), jnp.float32),
            pltpu.VMEM((TOKENS, 128), jnp.float32),
            pltpu.VMEM((TOKENS, 128), jnp.float32),
            pltpu.VMEM((D, QH * HD), jnp.bfloat16),
            pltpu.VMEM((D, KH * 2 * HD), jnp.bfloat16),
            pltpu.VMEM((QH * HD, D), jnp.bfloat16),
            pltpu.VMEM((ROWS, SLOTS, 128), jnp.bfloat16),
            pltpu.VMEM((4 * QH * ROWS, 128), jnp.float32),
            pltpu.VMEM((DRAFT * KH * ROWS, 128), jnp.float32),
            pltpu.VMEM((4 * QH * ROWS, 128), jnp.float32),
            pltpu.VMEM((4 * QH, SLOTS), jnp.float32),
            pltpu.VMEM((DRAFT, ROWS, D), jnp.bfloat16),
            pltpu.SemaphoreType.DMA((35,)),
        ],
        compiler_params=pltpu.CompilerParams(vmem_limit_bytes=VMEM_LIMIT),
        cost_estimate=pl.CostEstimate(flops=400_000_000, transcendentals=800_000, bytes_accessed=13_500_000),
        name="attend",
    )(lens, me, *pieces, gain, cosine, sine, wq, wkv, wo, kv)


def mlp_kernel(halves, tokens, gathered, out, weights, sems):
    copies = [
        pltpu.make_async_copy(gathered.at[h, z], weights.at[z, :, h], sems.at[2 * z + h])
        for z in range(Z)
        for h in range(2)
    ]
    for c in copies:
        c.start()
    count = tokens.shape[0]
    units = weights.shape[-1]
    gate = jnp.zeros((count, units), jnp.float32)
    up = jnp.zeros((count, units), jnp.float32)
    for z in range(Z):
        copies[2 * z].wait()
        copies[2 * z + 1].wait()
        part = tokens[:, z * 256 : (z + 1) * 256]
        gate = gate + jnp.dot(
            part, weights[z, :, :, 0:16, :].reshape(256, units), preferred_element_type=jnp.float32
        )
        up = up + jnp.dot(
            part, weights[z, :, :, 16:32, :].reshape(256, units), preferred_element_type=jnp.float32
        )
    act = (gate / (1.0 + jnp.exp(-gate)) * up).astype(jnp.bfloat16)
    for z in range(Z):
        down = weights[z, :, :, 32:48, :].reshape(256, units)
        share = lax.dot_general(
            act, down, (((1,), (1,)), ((), ())), preferred_element_type=jnp.float32
        ).astype(jnp.bfloat16)
        if halves:
            share = share.reshape(2, count // (2 * ROWS), ROWS, 256)
            at = (z % 4) * 256
            for side in range(2):
                out[z // 4, :, side, :, at : at + 256] = share[side]
        else:
            out[:, z * 256 : (z + 1) * 256] = share


def mlp(tokens, gathered, halves):
    hbm = pl.BlockSpec(memory_space=pltpu.HBM)
    vmem = pl.BlockSpec(memory_space=pltpu.VMEM)
    units = gathered.shape[-1]
    return pl.pallas_call(
        functools.partial(mlp_kernel, halves),
        out_shape=jax.ShapeDtypeStruct(
            (2, tokens.shape[0] // (2 * ROWS), 2, ROWS, D // 2) if halves else tokens.shape,
            jnp.bfloat16,
        ),
        in_specs=[vmem, hbm],
        out_specs=vmem,
        scratch_shapes=[
            pltpu.VMEM((Z, 8, 2, 48, units), jnp.bfloat16),
            pltpu.SemaphoreType.DMA((2 * Z,)),
        ],
        compiler_params=pltpu.CompilerParams(vmem_limit_bytes=VMEM_LIMIT),
        cost_estimate=pl.CostEstimate(flops=400_000_000, transcendentals=32768, bytes_accessed=4_200_000),
        name="mlp",
    )(tokens, gathered)


def after(first, then):
    return lax.optimization_barrier((first, then))[1]


def exchanged(blocks):
    return [
        lax.ppermute(blocks[k], CHIP, [(i, i ^ k) for i in range(4)]) for k in (1, 2, 3)
    ]


def normalize(hidden, gain):
    wide = hidden.astype(jnp.float32)
    factor = lax.rsqrt(jnp.mean(wide * wide, axis=-1, keepdims=True) + EPS)
    return (wide * factor * gain).astype(jnp.bfloat16)


def local(
    exit_hidden,
    exit_depth,
    context_len,
    attn_gain,
    w_query,
    w_keyval,
    w_out,
    kv_cache,
    mlp_gain,
    w_gate,
    w_up,
    w_down,
):
    section = lax.axis_index("section")
    tensor = lax.axis_index("tensor")

    def half_rows(which):
        return jnp.stack(
            [lax.dynamic_slice_in_dim(w[0], which * 16, 16, 0) for w in (w_gate, w_up, w_down)]
        )

    own_half = half_rows(section)
    got_half = lax.ppermute(half_rows(1 - section), "section", [(0, 1), (1, 0)])
    first = jnp.where(section == 0, own_half, got_half)
    second = jnp.where(section == 1, own_half, got_half)
    block0 = lax.all_to_all(
        first.reshape(3, 16, 8, FFS).transpose(2, 0, 1, 3).reshape(8, 48, FFS),
        ("y", "xh"),
        0,
        0,
        tiled=True,
    )

    other_gain = lax.ppermute(mlp_gain, "section", [(0, 1), (1, 0)])
    gains = [jnp.where(section == l, mlp_gain, other_gain) for l in range(2)]
    own_piece = exit_hidden.transpose(1, 0, 2)
    pieces = [own_piece] + exchanged([own_piece] * 4)

    def gathered(block):
        g = lax.all_gather(block, ("section", "z"), axis=0)
        return g.reshape(2, Z, 8, 48, block.shape[-1])

    weights = [gathered(after((pieces, other_gain), block0))]
    slices = second.reshape(3, 16, 4, 2 * FFS).transpose(2, 0, 1, 3).reshape(4, 1, 48, 2 * FFS)
    slices = jnp.broadcast_to(slices, (4, 2, 48, 2 * FFS)).reshape(8, 48, 2 * FFS)
    block1 = lax.all_to_all(after(pieces[3], slices), ("y", "xh"), 0, 0, tiled=True)

    where_at = (jnp.arange(DRAFT, dtype=jnp.int32)[:, None] + context_len[None, :]).reshape(TOKENS)
    rates = jnp.exp(jnp.arange(HD // 2, dtype=jnp.float32) * (-2.0 * math.log(THETA) / HD))
    angles = where_at.astype(jnp.float32)[:, None] * rates
    c = jnp.cos(angles)
    s = jnp.sin(angles)
    cosine = jnp.concatenate([c, c, c, c], axis=1)
    sine = jnp.concatenate([-s, s, -s, s], axis=1)

    cache = kv_cache[0].reshape(ROWS, SLOTS, 128)
    me = section * 2 + tensor
    for l in range(2):
        *partial, before, half = attend(
            l == 1,
            context_len,
            me.reshape(1),
            pieces,
            attn_gain,
            cosine,
            sine,
            w_query[0],
            w_keyval[0],
            w_out[0],
            cache,
        )
        near, across, far = exchanged(partial)
        mine = section == l
        mid = (
            before.astype(jnp.float32)
            + jnp.where(mine, partial[0], across).astype(jnp.float32)
            + jnp.where(mine, near, far).astype(jnp.float32)
        ).astype(jnp.bfloat16)
        if l == 0:
            weights.append(gathered(after(mid, block1)))
        mlp_in = normalize(mid, gains[l])
        axes, group = GROUPS[l]
        everyone = lax.all_to_all(
            jnp.broadcast_to(mlp_in[None], (group, ROWS, D)), axes, 0, 0, tiled=True
        )
        share = mlp(everyone.reshape(group * ROWS, D), weights[l], l == 1)
        if l == 0:
            shares = lax.all_to_all(share.reshape(group, ROWS, D), axes, 0, 0, tiled=True)
            total = jnp.sum(shares.astype(jnp.float32), axis=0)
            updated = (mid.astype(jnp.float32) + total).astype(jnp.bfloat16)
            kept = jnp.where((exit_depth <= l)[:, None], updated, before)
            pieces = [kept] + exchanged([kept] * 4)
    left, right = mid[:, : D // 2], mid[:, D // 2 :]
    same = jnp.where(tensor == 0, left, right)
    opposite = jnp.where(tensor == 0, right, left)
    got = lax.ppermute(opposite, "tensor", [(0, 1), (1, 0)])
    mids = jnp.where(tensor == 0, jnp.stack([same, got]), jnp.stack([got, same]))
    shares = lax.all_to_all(share.reshape(8, 2, ROWS, D // 2), axes, 0, 0, tiled=True)
    total = jnp.sum(shares.astype(jnp.float32), axis=0)
    updated = (mids.astype(jnp.float32) + total).astype(jnp.bfloat16)
    sent = lax.ppermute(updated, "section", [(0, 1)])
    last = jnp.concatenate([sent, updated])
    return jnp.where(section == 0, half, last).transpose(1, 0, 2)[None]


def solution(mesh):
    wide = Mesh(mesh.devices.reshape(2, 2, Z, 4, 2), ("section", "tensor", "z", "y", "xh"))
    dp = ("z", "y", "xh")
    in_specs = (
        P(dp, None, ("section", "tensor")),
        P(dp),
        P(dp),
        P("section", None),
        P("section", None, "tensor"),
        P("section", None, "tensor"),
        P("section", "tensor", None),
        P("section", dp, None, "tensor", None),
        P("section", None),
        P("section", dp, "tensor"),
        P("section", dp, "tensor"),
        P("section", dp, "tensor"),
    )
    out_specs = P("section", dp, None, "tensor")

    return jax.shard_map(local, mesh=wide, in_specs=in_specs, out_specs=out_specs, check_vma=False)
```

profile of v0, /device:TPU:1, one launch (start us, length us, event | category | flops | bytes accessed | tf_op | source)
XLA Modules:
  0.0 145.1 jit_solution(29827881717668543)
XLA Ops:
  6.5 0.9 constant_dynamic-slice_fusion.5
  7.4 1.0 constant_dynamic-slice_fusion.3
  8.4 3.3 %collective-permute-start.7 = (bf16[3,16,2048]{2,1,0:T(8,128)(2,1)S(1)}, bf16[3,16,2048]{2,1,0:T(8,128)(2,1)S(1)}, u32[]{:S(2)}, u32[]{:S(2)}) collective-permute-start(bf16[3,16,2048]{2,1,0:T(8,128)(2,1)S(1)} %pad_maximum_fusion.1), channel_id=1, source_target_pairs={{0,128},{128,0},{1,129},{129,1},{2,130},{130,2},{3,131},{131,3},{4... | collective-permute-start | bytes 589832 | tf_op jit(solution)/shard_map/ppermute | solution.py:312
  11.7 1.1 collective-permute-done.7
  12.8 0.7 copy.24
  13.5 4.9 %all-to-all-start.1 = ((bf16[8,48,256]{2,1,0:T(8,128)(2,1)}), bf16[8,48,256]{2,1,0:T(8,128)(2,1)S(1)}, u32[]{:S(2)}, u32[]{:S(2)}) async-start(bf16[8,48,256]{2,1,0:T(8,128)(2,1)} %bitcast.9), calls=%async_computation.1 | async-start | bytes 393216 | tf_op jit(solution)/shard_map/all_to_all | solution.py:315
  18.5 0.8 copy.25
  19.3 0.4 collective-permute-start
  19.7 0.9 collective-permute-start.1
  20.6 1.0 collective-permute-start.2
  21.7 0.5 collective-permute-start.6
  22.2 1.0 collective-permute-done.6
  23.2 1.0 collective-permute-done.2.refs_3_
  24.3 1.5 %all-to-all-done.1 = bf16[8,48,256]{2,1,0:T(8,128)(2,1)S(1)} async-done(((bf16[8,48,256]{2,1,0:T(8,128)(2,1)}), bf16[8,48,256]{2,1,0:T(8,128)(2,1)S(1)}, u32[]{:S(2)}, u32[]{:S(2)}) %all-to-all-start.1) | async-done | bytes 196640 | tf_op jit(solution)/shard_map/all_to_all | solution.py:315
  25.8 0.7 copy-done.3
  26.5 0.7 add_convert_fusion.3
  27.3 0.1 fusion.9
  27.6 0.8 broadcast_in_dim.22
  28.4 5.7 %all-to-all-start.4 = ((bf16[8,48,512]{2,1,0:T(8,128)(2,1)}), bf16[8,48,512]{2,1,0:T(8,128)(2,1)S(1)}, u32[]{:S(2)}, u32[]{:S(2)}) async-start(bf16[8,48,512]{2,1,0:T(8,128)(2,1)} %bitcast.18), calls=%async_computation.4 | async-start | bytes 786432 | tf_op jit(solution)/shard_map/all_to_all | solution.py:335
  34.2 9.0 %attend.2 = (bf16[8,2048]{1,0:T(8,128)(2,1)S(1)}, bf16[8,2048]{1,0:T(8,128)(2,1)S(1)}, bf16[8,2048]{1,0:T(8,128)(2,1)S(1)}, bf16[8,2048]{1,0:T(8,128)(2,1)S(1)},...) custom-call(s32[8]{0:T(128)S(1)} %copy-done.1, s32[1]{0:T(128)} %bitcast.me, bf16[4,8,512]{2,1,0:T(8,128)(2,1)S(1)} %bitcast.39, ...), custom_call_target="tpu_custom_call" | custom-call | flops 400000000 | bytes 13500000 | tf_op jit(solution)/shard_map/attend/pallas_call | solution.py:187
  43.4 1.9 %collective-permute-start.5 = (bf16[8,2048]{1,0:T(8,128)(2,1)S(1)}, bf16[8,2048]{1,0:T(8,128)(2,1)S(1)}, u32[]{:S(2)}, u32[]{:S(2)}) collective-permute-start(bf16[8,2048]{1,0:T(8,128)(2,1)S(1)} %get-tuple-element.23), channel_id=1, source_target_pairs={{0,192},{64,128},{128,64},{192,0},{1,193},{65,129},{129,65},{193,1... | collective-permute-start | bytes 98312 | tf_op jit(solution)/shard_map/ppermute | solution.py:279
  45.3 1.2 collective-permute-done.4
  46.5 1.2 collective-permute-done.5
  47.7 0.1 fusion.3
  47.9 0.8 copy-done.2
  48.8 16.7 %all_to_all.30 = bf16[16,8,2048]{2,1,0:T(8,128)(2,1)S(1)} all-to-all(bf16[16,8,2048]{2,1,0:T(8,128)(2,1)S(1)} %broadcast_in_dim.19), channel_id=1, replica_groups=mesh['section'=2,'tensor'=2,'z'=8,'y'=4,'xh'=2] {'tensor','y','xh'}, dimensions={0} | all-to-all | bytes 1048576 | tf_op jit(solution)/shard_map/all_to_all | solution.py:372
  65.5 3.7 %all-gather.5.cloned.1.call-done = bf16[128,48,256]{2,1,0:T(8,128)(2,1)} async-done(((bf16[8,48,256]{2,1,0:T(8,128)(2,1)}), bf16[128,48,256]{2,1,0:T(8,128)(2,1)}) %all-gather.5.cloned.1.call-update) | async-done | bytes 3145744 | tf_op jit(solution)/shard_map/all_gather | solution.py:329
  69.2 3.4 %mlp.2 = bf16[128,2048]{1,0:T(8,128)(2,1)} custom-call(bf16[128,2048]{1,0:T(8,128)(2,1)S(1)} %bitcast.34, bf16[2,8,8,48,256]{4,3,2,1,0:T(8,128)(2,1)} %bitcast.49), custom_call_target="tpu_custom_call" | custom-call | flops 400000000 | bytes 4200000 | tf_op jit(solution)/shard_map/mlp/pallas_call | solution.py:255
  72.6 6.4 %all-to-all-start.2 = ((bf16[16,8,2048]{2,1,0:T(8,128)(2,1)}), bf16[16,8,2048]{2,1,0:T(8,128)(2,1)S(1)}, u32[]{:S(2)}, u32[]{:S(2)}) async-start(bf16[16,8,2048]{2,1,0:T(8,128)(2,1)} %bitcast.11), calls=%async_computation.2 | async-start | bytes 1048576 | tf_op jit(solution)/shard_map/all_to_all | solution.py:377
  79.1 9.6 %all-to-all-done.2 = bf16[16,8,2048]{2,1,0:T(8,128)(2,1)S(1)} async-done(((bf16[16,8,2048]{2,1,0:T(8,128)(2,1)}), bf16[16,8,2048]{2,1,0:T(8,128)(2,1)S(1)}, u32[]{:S(2)}, u32[]{:S(2)}) %all-to-all-start.2) | async-done | bytes 524320 | tf_op jit(solution)/shard_map/all_to_all | solution.py:377
  88.8 0.4 collective-permute-start.8
  89.2 2.6 %collective-permute-start.9 = (bf16[8,2048]{1,0:T(8,128)(2,1)S(1)}, bf16[8,2048]{1,0:T(8,128)(2,1)S(1)}, u32[]{:S(2)}, u32[]{:S(2)}) collective-permute-start(bf16[8,2048]{1,0:T(8,128)(2,1)S(1)} %fusion.8.refs_0_), channel_id=1, source_target_pairs={{0,128},{64,192},{128,0},{192,64},{1,129},{65,193},{129,1},{193,65... | collective-permute-start | bytes 98312 | tf_op jit(solution)/shard_map/ppermute | solution.py:279
  91.8 1.1 collective-permute-start.10
  92.9 2.7 %collective-permute-done.10.refs_3_ = bf16[8,2048]{1,0:T(8,128)(2,1)S(1)} collective-permute-done((bf16[8,2048]{1,0:T(8,128)(2,1)S(1)}, bf16[8,2048]{1,0:T(8,128)(2,1)S(1)}, u32[]{:S(2)}, u32[]{:S(2)}) %collective-permute-start.10) | collective-permute-done | bytes 32800 | tf_op jit(solution)/shard_map/ppermute | solution.py:279
  95.6 9.1 %attend.3 = (bf16[8,2048]{1,0:T(8,128)(2,1)S(1)}, bf16[8,2048]{1,0:T(8,128)(2,1)S(1)}, bf16[8,2048]{1,0:T(8,128)(2,1)S(1)}, bf16[8,2048]{1,0:T(8,128)(2,1)S(1)},...) custom-call(s32[8]{0:T(128)S(1)} %copy-done.1, s32[1]{0:T(128)} %bitcast.me, ...), custom_call_target="tpu_custom_call" | custom-call | flops 400000000 | bytes 13500000 | tf_op jit(solution)/shard_map/attend/pallas_call | solution.py:187
  104.7 1.2 collective-permute-start.12
  106.0 0.4 collective-permute-start.13
  106.4 0.3 collective-permute-start.11
  106.7 1.3 collective-permute-done.12
  108.0 1.7 %collective-permute-done.13 = bf16[8,2048]{1,0:T(8,128)(2,1)S(1)} collective-permute-done((bf16[8,2048]{1,0:T(8,128)(2,1)S(1)}, bf16[8,2048]{1,0:T(8,128)(2,1)S(1)}, u32[]{:S(2)}, u32[]{:S(2)}) %collective-permute-start.13) | collective-permute-done | bytes 32800 | tf_op jit(solution)/shard_map/ppermute | solution.py:279
  110.0 8.6 %all_to_all.31 = bf16[8,8,2048]{2,1,0:T(8,128)(2,1)S(1)} all-to-all(bf16[8,8,2048]{2,1,0:T(8,128)(2,1)S(1)} %broadcast_in_dim.20), channel_id=1, replica_groups=mesh['section'=2,'tensor'=2,'z'=8,'y'=4,'xh'=2] {'tensor','y'}, dimensions={0} | all-to-all | bytes 524288 | tf_op jit(solution)/shard_map/all_to_all | solution.py:372
  118.6 4.5 %mlp.3 = bf16[2,4,2,8,1024]{4,3,2,1,0:T(8,128)(2,1)} custom-call(bf16[64,2048]{1,0:T(8,128)(2,1)S(1)} %bitcast.35, bf16[2,8,8,48,512]{4,3,2,1,0:T(8,128)(2,1)} %bitcast.48), custom_call_target="tpu_custom_call" | custom-call | flops 400000000 | bytes 4200000 | tf_op jit(solution)/shard_map/mlp/pallas_call | solution.py:255
  123.1 4.1 %all-to-all-start.5 = ((bf16[8,2,8,1024]{3,2,1,0:T(8,128)(2,1)}), bf16[8,2,8,1024]{3,2,1,0:T(8,128)(2,1)S(1)}, u32[]{:S(2)}, u32[]{:S(2)}) async-start(bf16[8,2,8,1024]{3,2,1,0:T(8,128)(2,1)} %bitcast.20), calls=%async_computation.5 | async-start | bytes 524288 | tf_op jit(solution)/shard_map/all_to_all | solution.py:387
  127.1 1.5 %collective-permute-start.14 = (bf16[8,1024]{1,0:T(8,128)(2,1)S(1)}, bf16[8,1024]{1,0:T(8,128)(2,1)S(1)}, u32[]{:S(2)}, u32[]{:S(2)}) collective-permute-start(bf16[8,1024]{1,0:T(8,128)(2,1)S(1)} %get-tuple-element.46), channel_id=1, source_target_pairs={{0,64},{64,0},{1,65},{65,1},{2,66},{66,2},{3,67},{67,3},{4,68},{68... | collective-permute-start | bytes 49160 | tf_op jit(solution)/shard_map/ppermute | solution.py:385
  128.7 4.6 %all-to-all-done.5 = bf16[8,2,8,1024]{3,2,1,0:T(8,128)(2,1)S(1)} async-done(((bf16[8,2,8,1024]{3,2,1,0:T(8,128)(2,1)}), bf16[8,2,8,1024]{3,2,1,0:T(8,128)(2,1)S(1)}, u32[]{:S(2)}, u32[]{:S(2)}) %all-to-all-start.5) | async-done | bytes 262176 | tf_op jit(solution)/shard_map/all_to_all | solution.py:387
  133.3 1.3 collective-permute-start.15
  134.6 2.9 %collective-permute-done.15 = bf16[2,8,1024]{2,1,0:T(8,128)(2,1)S(1)} collective-permute-done((bf16[2,8,1024]{2,1,0:T(8,128)(2,1)S(1)}, bf16[2,8,1024]{2,1,0:T(8,128)(2,1)S(1)}, u32[]{:S(2)}, u32[]{:S(2)}) %collective-permute-start.15) | collective-permute-done | bytes 32800 | tf_op jit(solution)/shard_map/ppermute | solution.py:390
  137.6 0.7 copy.20
  (47 shorter events, 1.3 us)
Async XLA Ops:
  6.5 27.7 %copy-start.1 = (s32[8]{0:T(128)S(1)}, s32[8]{0:T(128)}, u32[]{:S(2)}) copy-start(s32[8]{0:T(128)} %lens.3) | copy-start | bytes 100
  6.5 27.7 %copy-start = (f32[1,2048]{1,0:T(1,128)S(1)}, f32[1,2048]{1,0:T(1,128)}, u32[]{:S(2)}) copy-start(f32[1,2048]{1,0:T(1,128)} %refs_4_.3) | copy-start | bytes 24580
  8.4 4.4 %collective-permute-start.7 = (bf16[3,16,2048]{2,1,0:T(8,128)(2,1)S(1)}, bf16[3,16,2048]{2,1,0:T(8,128)(2,1)S(1)}, u32[]{:S(2)}, u32[]{:S(2)}) collective-permute-start(bf16[3,16,2048]{2,1,0:T(8,128)(2,1)S(1)} %pad_maximum_fusion.1), channel_id=1, source_target_pairs={{0,128},{128,0},{1,129},{129,1},{2,130},{130,2},{3,131},{131,3},{4... | collective-permute-start | bytes 589832 | tf_op jit(solution)/shard_map/ppermute | solution.py:312
  13.5 12.3 %all-to-all-start.1 = ((bf16[8,48,256]{2,1,0:T(8,128)(2,1)}), bf16[8,48,256]{2,1,0:T(8,128)(2,1)S(1)}, u32[]{:S(2)}, u32[]{:S(2)}) async-start(bf16[8,48,256]{2,1,0:T(8,128)(2,1)} %bitcast.9), calls=%async_computation.1 | async-start | bytes 393216 | tf_op jit(solution)/shard_map/all_to_all | solution.py:315
  18.5 50.7 %all-gather.5.cloned.1.call-start = ((), (), s32[]{:S(2)}) async-start(), calls=%async_computation.6 | async-start | bytes 3342336 | tf_op jit(solution)/shard_map/all_gather | solution.py:329
  19.3 3.9 %collective-permute-start = (bf16[4,8,512]{2,1,0:T(8,128)(2,1)S(1)}, bf16[4,8,512]{2,1,0:T(8,128)(2,1)S(1)}, u32[]{:S(2)}, u32[]{:S(2)}) collective-permute-start(bf16[4,8,512]{2,1,0:T(8,128)(2,1)S(1)} %bitcast.36), channel_id=1, source_target_pairs={{0,64},{64,0},{128,192},{192,128},{1,65},{65,1},{129,193},{193,129... | collective-permute-start | bytes 98312 | tf_op jit(solution)/shard_map/ppermute | solution.py:279
  19.7 3.5 %collective-permute-start.1 = (bf16[4,8,512]{2,1,0:T(8,128)(2,1)S(1)}, bf16[4,8,512]{2,1,0:T(8,128)(2,1)S(1)}, u32[]{:S(2)}, u32[]{:S(2)}) collective-permute-start(bf16[4,8,512]{2,1,0:T(8,128)(2,1)S(1)} %bitcast.37), channel_id=1, source_target_pairs={{0,128},{64,192},{128,0},{192,64},{1,129},{65,193},{129,1},{193,65... | collective-permute-start | bytes 98312 | tf_op jit(solution)/shard_map/ppermute | solution.py:279
  20.6 3.6 %collective-permute-start.2 = (bf16[4,8,512]{2,1,0:T(8,128)(2,1)S(1)}, bf16[4,8,512]{2,1,0:T(8,128)(2,1)S(1)}, u32[]{:S(2)}, u32[]{:S(2)}) collective-permute-start(bf16[4,8,512]{2,1,0:T(8,128)(2,1)S(1)} %bitcast.38), channel_id=1, source_target_pairs={{0,192},{64,128},{128,64},{192,0},{1,193},{65,129},{129,65},{193,1... | collective-permute-start | bytes 98312 | tf_op jit(solution)/shard_map/ppermute | solution.py:279
  21.7 1.5 %collective-permute-start.6 = (f32[1,2048]{1,0:T(1,128)}, f32[1,2048]{1,0:T(1,128)S(1)}, u32[]{:S(2)}, u32[]{:S(2)}) collective-permute-start(f32[1,2048]{1,0:T(1,128)} %param.20), channel_id=1, source_target_pairs={{0,128},{128,0},{1,129},{129,1},{2,130},{130,2},{3,131},{131,3},{4... | collective-permute-start | bytes 24584 | tf_op jit(solution)/shard_map/ppermute | solution.py:323
  25.8 0.7 copy-start.3
  28.4 19.5 %all-to-all-start.4 = ((bf16[8,48,512]{2,1,0:T(8,128)(2,1)}), bf16[8,48,512]{2,1,0:T(8,128)(2,1)S(1)}, u32[]{:S(2)}, u32[]{:S(2)}) async-start(bf16[8,48,512]{2,1,0:T(8,128)(2,1)} %bitcast.18), calls=%async_computation.4 | async-start | bytes 786432 | tf_op jit(solution)/shard_map/all_to_all | solution.py:335
  34.0 84.5 %all-gather.7.cloned.1.call-start = ((), (), s32[]{:S(2)}) async-start(), calls=%async_computation.7 | async-start | bytes 6684672 | tf_op jit(solution)/shard_map/all_gather | solution.py:329
  34.2 14.4 %copy-start.4 = (f32[1,2048]{1,0:T(1,128)S(1)}, f32[1,2048]{1,0:T(1,128)}, u32[]{:S(2)}) copy-start(f32[1,2048]{1,0:T(1,128)} %param.20) | copy-start | bytes 24580
  43.2 35.8 %copy-start.5 = (s32[8]{0:T(128)S(1)}, s32[8]{0:T(128)}, u32[]{:S(2)}) copy-start(s32[8]{0:T(128)} %param.13) | copy-start | bytes 100
  43.3 3.3 %collective-permute-start.4 = (bf16[8,2048]{1,0:T(8,128)(2,1)S(1)}, bf16[8,2048]{1,0:T(8,128)(2,1)S(1)}, u32[]{:S(2)}, u32[]{:S(2)}) collective-permute-start(bf16[8,2048]{1,0:T(8,128)(2,1)S(1)} %get-tuple-element.22), channel_id=1, source_target_pairs={{0,64},{64,0},{128,192},{192,128},{1,65},{65,1},{129,193},{193,129... | collective-permute-start | bytes 98312 | tf_op jit(solution)/shard_map/ppermute | solution.py:279
  43.4 4.3 %collective-permute-start.5 = (bf16[8,2048]{1,0:T(8,128)(2,1)S(1)}, bf16[8,2048]{1,0:T(8,128)(2,1)S(1)}, u32[]{:S(2)}, u32[]{:S(2)}) collective-permute-start(bf16[8,2048]{1,0:T(8,128)(2,1)S(1)} %get-tuple-element.23), channel_id=1, source_target_pairs={{0,192},{64,128},{128,64},{192,0},{1,193},{65,129},{129,65},{193,1... | collective-permute-start | bytes 98312 | tf_op jit(solution)/shard_map/ppermute | solution.py:279
  45.3 2.4 %collective-permute-start.3 = (bf16[8,2048]{1,0:T(8,128)(2,1)S(1)}, bf16[8,2048]{1,0:T(8,128)(2,1)S(1)}, u32[]{:S(2)}, u32[]{:S(2)}) collective-permute-start(bf16[8,2048]{1,0:T(8,128)(2,1)S(1)} %get-tuple-element.21), channel_id=1, source_target_pairs={{0,128},{64,192},{128,0},{192,64},{1,129},{65,193},{129,1},{193,65... | collective-permute-start | bytes 98312 | tf_op jit(solution)/shard_map/ppermute | solution.py:279
  47.8 0.8 copy-start.2
  72.6 16.0 %all-to-all-start.2 = ((bf16[16,8,2048]{2,1,0:T(8,128)(2,1)}), bf16[16,8,2048]{2,1,0:T(8,128)(2,1)S(1)}, u32[]{:S(2)}, u32[]{:S(2)}) async-start(bf16[16,8,2048]{2,1,0:T(8,128)(2,1)} %bitcast.11), calls=%async_computation.2 | async-start | bytes 1048576 | tf_op jit(solution)/shard_map/all_to_all | solution.py:377
  88.8 4.1 %collective-permute-start.8 = (bf16[8,2048]{1,0:T(8,128)(2,1)S(1)}, bf16[8,2048]{1,0:T(8,128)(2,1)S(1)}, u32[]{:S(2)}, u32[]{:S(2)}) collective-permute-start(bf16[8,2048]{1,0:T(8,128)(2,1)S(1)} %fusion.8.refs_0_), channel_id=1, source_target_pairs={{0,64},{64,0},{128,192},{192,128},{1,65},{65,1},{129,193},{193,129... | collective-permute-start | bytes 98312 | tf_op jit(solution)/shard_map/ppermute | solution.py:279
  89.2 3.7 %collective-permute-start.9 = (bf16[8,2048]{1,0:T(8,128)(2,1)S(1)}, bf16[8,2048]{1,0:T(8,128)(2,1)S(1)}, u32[]{:S(2)}, u32[]{:S(2)}) collective-permute-start(bf16[8,2048]{1,0:T(8,128)(2,1)S(1)} %fusion.8.refs_0_), channel_id=1, source_target_pairs={{0,128},{64,192},{128,0},{192,64},{1,129},{65,193},{129,1},{193,65... | collective-permute-start | bytes 98312 | tf_op jit(solution)/shard_map/ppermute | solution.py:279
  91.8 3.8 %collective-permute-start.10 = (bf16[8,2048]{1,0:T(8,128)(2,1)S(1)}, bf16[8,2048]{1,0:T(8,128)(2,1)S(1)}, u32[]{:S(2)}, u32[]{:S(2)}) collective-permute-start(bf16[8,2048]{1,0:T(8,128)(2,1)S(1)} %fusion.8.refs_0_), channel_id=1, source_target_pairs={{0,192},{64,128},{128,64},{192,0},{1,193},{65,129},{129,65},{193,1... | collective-permute-start | bytes 98312 | tf_op jit(solution)/shard_map/ppermute | solution.py:279
  104.7 3.3 %collective-permute-start.12 = (bf16[8,2048]{1,0:T(8,128)(2,1)S(1)}, bf16[8,2048]{1,0:T(8,128)(2,1)S(1)}, u32[]{:S(2)}, u32[]{:S(2)}) collective-permute-start(bf16[8,2048]{1,0:T(8,128)(2,1)S(1)} %get-tuple-element.29), channel_id=1, source_target_pairs={{0,64},{64,0},{128,192},{192,128},{1,65},{65,1},{129,193},{193,129... | collective-permute-start | bytes 98312 | tf_op jit(solution)/shard_map/ppermute | solution.py:279
  106.0 3.7 %collective-permute-start.13 = (bf16[8,2048]{1,0:T(8,128)(2,1)S(1)}, bf16[8,2048]{1,0:T(8,128)(2,1)S(1)}, u32[]{:S(2)}, u32[]{:S(2)}) collective-permute-start(bf16[8,2048]{1,0:T(8,128)(2,1)S(1)} %get-tuple-element.30), channel_id=1, source_target_pairs={{0,192},{64,128},{128,64},{192,0},{1,193},{65,129},{129,65},{193,1... | collective-permute-start | bytes 98312 | tf_op jit(solution)/shard_map/ppermute | solution.py:279
  106.4 3.3 %collective-permute-start.11 = (bf16[8,2048]{1,0:T(8,128)(2,1)S(1)}, bf16[8,2048]{1,0:T(8,128)(2,1)S(1)}, u32[]{:S(2)}, u32[]{:S(2)}) collective-permute-start(bf16[8,2048]{1,0:T(8,128)(2,1)S(1)} %get-tuple-element.28), channel_id=1, source_target_pairs={{0,128},{64,192},{128,0},{192,64},{1,129},{65,193},{129,1},{193,65... | collective-permute-start | bytes 98312 | tf_op jit(solution)/shard_map/ppermute | solution.py:279
  123.1 10.2 %all-to-all-start.5 = ((bf16[8,2,8,1024]{3,2,1,0:T(8,128)(2,1)}), bf16[8,2,8,1024]{3,2,1,0:T(8,128)(2,1)S(1)}, u32[]{:S(2)}, u32[]{:S(2)}) async-start(bf16[8,2,8,1024]{3,2,1,0:T(8,128)(2,1)} %bitcast.20), calls=%async_computation.5 | async-start | bytes 524288 | tf_op jit(solution)/shard_map/all_to_all | solution.py:387
  127.1 6.2 %collective-permute-start.14 = (bf16[8,1024]{1,0:T(8,128)(2,1)S(1)}, bf16[8,1024]{1,0:T(8,128)(2,1)S(1)}, u32[]{:S(2)}, u32[]{:S(2)}) collective-permute-start(bf16[8,1024]{1,0:T(8,128)(2,1)S(1)} %get-tuple-element.46), channel_id=1, source_target_pairs={{0,64},{64,0},{1,65},{65,1},{2,66},{66,2},{3,67},{67,3},{4,68},{68... | collective-permute-start | bytes 49160 | tf_op jit(solution)/shard_map/ppermute | solution.py:385
  133.3 4.2 %collective-permute-start.15 = (bf16[2,8,1024]{2,1,0:T(8,128)(2,1)S(1)}, bf16[2,8,1024]{2,1,0:T(8,128)(2,1)S(1)}, u32[]{:S(2)}, u32[]{:S(2)}) collective-permute-start(bf16[2,8,1024]{2,1,0:T(8,128)(2,1)S(1)} %add_convert_fusion), channel_id=1, source_target_pairs={{0,128},{1,129},{2,130},{3,131},{4,132},{5,133},{6,134},{7,135},{8... | collective-permute-start | bytes 98312 | tf_op jit(solution)/shard_map/ppermute | solution.py:390
Sparse Core Ops, SparseCore 0:
  26.6 42.5 all-gather.4
  71.0 44.5 all-gather.6
where the time goes:
time: 146 us; the launch traced here: 145 us
  starting transfers between devices  38.2 us (26%)
  waiting for transfers between devices  33.7 us (23%)
  Pallas kernels  26.1 us (18%)
  blocking collectives  25.2 us (17%)
  between operations  13.7 us (9%)
  local copies, waits for them, and re-layouts  6.58 us (5%)
  other arithmetic  1.67 us (1%)
    all_to_all x2, blocking collectives, local(): lax.all_to_all(jnp.broadcast_to(mlp_in[None], (group, ROWS, D)), axes, 0,...  25.2 us
    pallas_call x2, Pallas kernels, attend(): pl.pallas_call(functools.partial(attend_kernel, by_token), out_shape=[qua...  18.2 us
    ppermute x12, starting transfers between devices, exchanged(): lax.ppermute(blocks[k], CHIP, [(i, i ^ k) for i in range(4)])  10.4 us
    all_to_all x1, waiting for transfers between devices, local(): lax.all_to_all(share.reshape(group, ROWS, D), axes, 0, 0, tiled=True)  9.59 us
    ppermute x12, waiting for transfers between devices, exchanged(): lax.ppermute(blocks[k], CHIP, [(i, i ^ k) for i in range(4)])  9.2 us
    pallas_call x2, Pallas kernels, mlp(): pl.pallas_call(functools.partial(mlp_kernel, halves), out_shape=jax.Shape...  7.93 us
    all_to_all x1, starting transfers between devices, local(): lax.all_to_all(share.reshape(group, ROWS, D), axes, 0, 0, tiled=True)  6.41 us
    all_to_all x1, starting transfers between devices, local(): lax.all_to_all(after(pieces[3], slices), ('y', 'xh'), 0, 0, tiled=True)  5.66 us
  transfers between devices with their start and end apart: 22, of which 13 were waited for; matrix products, arithmetic and copies ran while one was open for 2% of the time, Pallas kernels for 15%

commit v1 on v0

--- a/solution.py
+++ b/solution.py
@@ -19,7 +19,7 @@
 KH = 4
 SLOTS = CTX * KH
 VMEM_LIMIT = 53000 * 1024
-AHEAD = 5
+AHEAD = 8
 FFS = 256
 EPS = 1e-05
 THETA = 500000.0
@@ -36,7 +36,7 @@
     gain_h, cos_h, sin_h, wq_h, wkv_h, wo_h, kv_h, *refs = refs
     out, refs = refs[:4], refs[4:]
     kept, half, *refs = refs
-    hidden, gain, cosine, sine, wq, wkv, wo, kv, qs, nk, hs, bias, result, sems = refs
+    hidden, gain, cosine, sine, wq, wkv, wo, kv, qs, nk, hs, slot, result, sems = refs
     mine = me[0]
     small = []
     small.append(pltpu.make_async_copy(gain_h, gain, sems.at[4]))
@@ -78,7 +78,7 @@
 
     row = lax.broadcasted_iota(jnp.int32, (4 * QH, SLOTS), 0)
     place = lax.broadcasted_iota(jnp.int32, (4 * QH, SLOTS), 1)
-    bias[...] = jnp.where((place & 3) == (row >> 4), 0.0, NEGATIVE)
+    slot[...] = jnp.where((place & 3) == (row >> 4), place, SLOTS)
     new_row = lax.broadcasted_iota(jnp.int32, (4 * QH, DRAFT * KH), 0)
     new_col = lax.broadcasted_iota(jnp.int32, (4 * QH, DRAFT * KH), 1)
     seen = ((new_col & 3) == (new_row >> 4)) & ((new_col >> 2) <= (new_row & 3))
@@ -140,7 +140,7 @@
             arrived(chunks + r // 2)
         stored = kv[r]
         scores = lax.dot_general(asked, stored, last, preferred_element_type=jnp.float32)
-        scores = jnp.where(place < KH * lens[r], scores, NEGATIVE) + bias[...]
+        scores = jnp.where(slot[...] < KH * lens[r], scores, NEGATIVE)
         new_scores = lax.dot_general(asked, fresh, last, preferred_element_type=jnp.float32)
         new_scores = jnp.where(seen, new_scores, NEGATIVE)
         top = jnp.maximum(
@@ -201,7 +201,7 @@
             pltpu.VMEM((4 * QH * ROWS, 128), jnp.float32),
             pltpu.VMEM((DRAFT * KH * ROWS, 128), jnp.float32),
             pltpu.VMEM((4 * QH * ROWS, 128), jnp.float32),
-            pltpu.VMEM((4 * QH, SLOTS), jnp.float32),
+            pltpu.VMEM((4 * QH, SLOTS), jnp.int32),
             pltpu.VMEM((DRAFT, ROWS, D), jnp.bfloat16),
             pltpu.SemaphoreType.DMA((35,)),
         ],
@@ -212,10 +212,16 @@
 
 
 def mlp_kernel(halves, tokens, gathered, out, weights, sems):
+    parts = gathered.shape[3]
     copies = [
-        pltpu.make_async_copy(gathered.at[h, z], weights.at[z, :, h], sems.at[2 * z + h])
+        pltpu.make_async_copy(
+            gathered.at[h, z, :, part],
+            weights.at[z, :, h, :, pl.ds(part * FFS, FFS)],
+            sems.at[(2 * z + h) * parts + part],
+        )
         for z in range(Z)
         for h in range(2)
+        for part in range(parts)
     ]
     for c in copies:
         c.start()
@@ -224,8 +230,8 @@
     gate = jnp.zeros((count, units), jnp.float32)
     up = jnp.zeros((count, units), jnp.float32)
     for z in range(Z):
-        copies[2 * z].wait()
-        copies[2 * z + 1].wait()
+        for c in copies[2 * z * parts : 2 * (z + 1) * parts]:
+            c.wait()
         part = tokens[:, z * 256 : (z + 1) * 256]
         gate = gate + jnp.dot(
             part, weights[z, :, :, 0:16, :].reshape(256, units), preferred_element_type=jnp.float32
@@ -251,7 +257,7 @@
 def mlp(tokens, gathered, halves):
     hbm = pl.BlockSpec(memory_space=pltpu.HBM)
     vmem = pl.BlockSpec(memory_space=pltpu.VMEM)
-    units = gathered.shape[-1]
+    units = gathered.shape[3] * FFS
     return pl.pallas_call(
         functools.partial(mlp_kernel, halves),
         out_shape=jax.ShapeDtypeStruct(
@@ -262,12 +268,32 @@
         out_specs=vmem,
         scratch_shapes=[
             pltpu.VMEM((Z, 8, 2, 48, units), jnp.bfloat16),
-            pltpu.SemaphoreType.DMA((2 * Z,)),
+            pltpu.SemaphoreType.DMA((2 * Z * gathered.shape[3],)),
         ],
         compiler_params=pltpu.CompilerParams(vmem_limit_bytes=VMEM_LIMIT),
         cost_estimate=pl.CostEstimate(flops=400_000_000, transcendentals=32768, bytes_accessed=4_200_000),
         name="mlp",
     )(tokens, gathered)
+
+
+def halves_kernel(section, gate, up, down, keep, give):
+    for out, which in ((keep, section[0]), (give, 1 - section[0])):
+        at = pl.ds(pl.multiple_of(which * 16, 16), 16)
+        for g, w in enumerate((gate, up, down)):
+            for a in range(8):
+                out[a, g * 16 : (g + 1) * 16, :] = w[at, a * FFS : (a + 1) * FFS]
+
+
+def laid_halves(section, gate, up, down):
+    vmem = pl.BlockSpec(memory_space=pltpu.VMEM)
+    return pl.pallas_call(
+        halves_kernel,
+        out_shape=[jax.ShapeDtypeStruct((8, 48, FFS), jnp.bfloat16)] * 2,
+        in_specs=[pl.BlockSpec(memory_space=pltpu.SMEM), vmem, vmem, vmem],
+        out_specs=[vmem, vmem],
+        compiler_params=pltpu.CompilerParams(vmem_limit_bytes=VMEM_LIMIT),
+        name="halves",
+    )(section, gate, up, down)
 
 
 def after(first, then):
@@ -303,22 +329,11 @@
     section = lax.axis_index("section")
     tensor = lax.axis_index("tensor")
 
-    def half_rows(which):
-        return jnp.stack(
-            [lax.dynamic_slice_in_dim(w[0], which * 16, 16, 0) for w in (w_gate, w_up, w_down)]
-        )
-
-    own_half = half_rows(section)
-    got_half = lax.ppermute(half_rows(1 - section), "section", [(0, 1), (1, 0)])
-    first = jnp.where(section == 0, own_half, got_half)
-    second = jnp.where(section == 1, own_half, got_half)
-    block0 = lax.all_to_all(
-        first.reshape(3, 16, 8, FFS).transpose(2, 0, 1, 3).reshape(8, 48, FFS),
-        ("y", "xh"),
-        0,
-        0,
-        tiled=True,
-    )
+    kept_half, sent_half = laid_halves(section.reshape(1), w_gate[0], w_up[0], w_down[0])
+    got_half = lax.ppermute(sent_half, "section", [(0, 1), (1, 0)])
+    first = jnp.where(section == 0, kept_half, got_half)
+    second = jnp.where(section == 1, kept_half, got_half)
+    block0 = lax.all_to_all(first, ("y", "xh"), 0, 0, tiled=True)
 
     other_gain = lax.ppermute(mlp_gain, "section", [(0, 1), (1, 0)])
     gains = [jnp.where(section == l, mlp_gain, other_gain) for l in range(2)]
@@ -327,11 +342,12 @@
 
     def gathered(block):
         g = lax.all_gather(block, ("section", "z"), axis=0)
-        return g.reshape(2, Z, 8, 48, block.shape[-1])
+        return g.reshape(2, Z, 8, -1, 48, FFS)
 
     weights = [gathered(after((pieces, other_gain), block0))]
-    slices = second.reshape(3, 16, 4, 2 * FFS).transpose(2, 0, 1, 3).reshape(4, 1, 48, 2 * FFS)
-    slices = jnp.broadcast_to(slices, (4, 2, 48, 2 * FFS)).reshape(8, 48, 2 * FFS)
+    slices = jnp.broadcast_to(
+        second.reshape(4, 1, 2, 48, FFS), (4, 2, 2, 48, FFS)
+    ).reshape(8, 2, 48, FFS)
     block1 = lax.all_to_all(after(pieces[3], slices), ("y", "xh"), 0, 0, tiled=True)
 
     where_at = (jnp.arange(DRAFT, dtype=jnp.int32)[:, None] + context_len[None, :]).reshape(TOKENS)

time: 146 us -> 147 us (level)
    unnamed x13 -> x23, local copies, waits for them, and re-layouts: 2.23 us -> 6.29 us
    dynamic_slice x2 -> x0, local copies, waits for them, and re-layouts: 1.87 us -> none  [half_rows(): lax.dynamic_slice_in_dim(w[0], which * 16, 16, 0)]
where the time goes in v1:
time: 147 us; the launch traced here: 146 us
  starting transfers between devices  38.4 us (26%)
  waiting for transfers between devices  32.9 us (22%)
  Pallas kernels  26.2 us (18%)
  blocking collectives  25 us (17%)
  between operations  13.6 us (9%)
  local copies, waits for them, and re-layouts  7.91 us (5%)
  other arithmetic  2.3 us (2%)
    all_to_all x2, blocking collectives, local(): lax.all_to_all(jnp.broadcast_to(mlp_in[None], (group, ROWS, D)), axes, 0,...  25 us
    pallas_call x2, Pallas kernels, attend(): pl.pallas_call(functools.partial(attend_kernel, by_token), out_shape=[qua...  17.9 us
    ppermute x12, starting transfers between devices, exchanged(): lax.ppermute(blocks[k], CHIP, [(i, i ^ k) for i in range(4)])  10.4 us
    all_to_all x1, waiting for transfers between devices, local(): lax.all_to_all(share.reshape(group, ROWS, D), axes, 0, 0, tiled=True)  9.59 us
    ppermute x12, waiting for transfers between devices, exchanged(): lax.ppermute(blocks[k], CHIP, [(i, i ^ k) for i in range(4)])  9.22 us
    pallas_call x2, Pallas kernels, mlp(): pl.pallas_call(functools.partial(mlp_kernel, halves), out_shape=jax.Shape...  8.2 us
    all_to_all x1, starting transfers between devices, local(): lax.all_to_all(share.reshape(group, ROWS, D), axes, 0, 0, tiled=True)  6.63 us
    unnamed x23, local copies, waits for them, and re-layouts  6.29 us
  transfers between devices with their start and end apart: 22, of which 13 were waited for; matrix products, arithmetic and copies ran while one was open for 2% of the time, Pallas kernels for 15%

profile of v1, /device:TPU:1, one launch (start us, length us, event | category | flops | bytes accessed | tf_op | source)
XLA Modules:
  0.0 146.3 jit_solution(6469408956710580308)
XLA Ops:
  6.5 0.9 copy-done
  7.4 0.9 copy-done.1
  8.3 0.9 copy-done.2
  9.3 3.3 %collective-permute-start.7 = (bf16[8,48,256]{2,1,0:T(8,128)(2,1)S(1)}, bf16[8,48,256]{2,1,0:T(8,128)(2,1)S(1)}, u32[]{:S(2)}, u32[]{:S(2)}) collective-permute-start(bf16[8,48,256]{2,1,0:T(8,128)(2,1)S(1)} %get-tuple-element.27), channel_id=1, source_target_pairs={{0,128},{128,0},{1,129},{129,1},{2,130},{130,2},{3,131},{131,3},{4... | collective-permute-start | bytes 589832 | tf_op jit(solution)/shard_map/ppermute | solution.py:333
  12.6 1.1 collective-permute-done.7
  13.6 0.7 broadcast_select_fusion
  14.3 4.9 %all-to-all-start.1 = ((bf16[8,48,256]{2,1,0:T(8,128)(2,1)}), bf16[8,48,256]{2,1,0:T(8,128)(2,1)S(1)}, u32[]{:S(2)}, u32[]{:S(2)}) async-start(bf16[8,48,256]{2,1,0:T(8,128)(2,1)} %get-tuple-element.42), calls=%async_computation.1 | async-start | bytes 393216 | tf_op jit(solution)/shard_map/all_to_all | solution.py:336
  19.3 0.8 copy.18
  20.1 0.4 collective-permute-start
  20.5 0.9 collective-permute-start.1
  21.4 1.0 collective-permute-start.2
  22.5 0.5 collective-permute-start.6
  23.0 1.0 collective-permute-done.6
  24.0 1.0 collective-permute-done.2.refs_3_
  25.1 1.5 %all-to-all-done.1 = bf16[8,48,256]{2,1,0:T(8,128)(2,1)S(1)} async-done(((bf16[8,48,256]{2,1,0:T(8,128)(2,1)}), bf16[8,48,256]{2,1,0:T(8,128)(2,1)S(1)}, u32[]{:S(2)}, u32[]{:S(2)}) %all-to-all-start.1) | async-done | bytes 196640 | tf_op jit(solution)/shard_map/all_to_all | solution.py:336
  26.6 0.7 copy-done.8
  27.3 0.7 add_convert_fusion.3
  28.2 0.8 broadcast_in_dim.22
  29.0 5.7 %all-to-all-start.4 = ((bf16[8,2,48,256]{3,2,1,0:T(8,128)(2,1)}), bf16[8,2,48,256]{3,2,1,0:T(8,128)(2,1)S(1)}, u32[]{:S(2)}, u32[]{:S(2)}) async-start(bf16[8,2,48,256]{3,2,1,0:T(8,128)(2,1)} %bitcast.19), calls=%async_computation.4 | async-start | bytes 786432 | tf_op jit(solution)/shard_map/all_to_all | solution.py:351
  34.8 0.7 copy-done.3
  35.5 0.7 copy-done.5
  36.2 8.9 %attend.2 = (bf16[8,2048]{1,0:T(8,128)(2,1)S(1)}, bf16[8,2048]{1,0:T(8,128)(2,1)S(1)}, bf16[8,2048]{1,0:T(8,128)(2,1)S(1)}, bf16[8,2048]{1,0:T(8,128)(2,1)S(1)},...) custom-call(s32[8]{0:T(128)S(1)} %copy-done.5, s32[1]{0:T(128)} %bitcast.me, bf16[4,8,512]{2,1,0:T(8,128)(2,1)S(1)} %bitcast.34, ...), custom_call_target="tpu_custom_call" | custom-call | flops 400000000 | bytes 13500000 | tf_op jit(solution)/shard_map/attend/pallas_call | solution.py:187
  45.2 1.9 %collective-permute-start.5 = (bf16[8,2048]{1,0:T(8,128)(2,1)S(1)}, bf16[8,2048]{1,0:T(8,128)(2,1)S(1)}, u32[]{:S(2)}, u32[]{:S(2)}) collective-permute-start(bf16[8,2048]{1,0:T(8,128)(2,1)S(1)} %get-tuple-element.25), channel_id=1, source_target_pairs={{0,192},{64,128},{128,64},{192,0},{1,193},{65,129},{129,65},{193,1... | collective-permute-start | bytes 98312 | tf_op jit(solution)/shard_map/ppermute | solution.py:305
  47.1 1.3 collective-permute-done.4
  48.4 1.2 collective-permute-done.5
  49.7 0.8 copy-done.7
  50.7 16.4 %all_to_all.30 = bf16[16,8,2048]{2,1,0:T(8,128)(2,1)S(1)} all-to-all(bf16[16,8,2048]{2,1,0:T(8,128)(2,1)S(1)} %broadcast_in_dim.19), channel_id=1, replica_groups=mesh['section'=2,'tensor'=2,'z'=8,'y'=4,'xh'=2] {'tensor','y','xh'}, dimensions={0} | all-to-all | bytes 1048576 | tf_op jit(solution)/shard_map/all_to_all | solution.py:388
  67.1 2.9 %all-gather.5.cloned.1.call-done = bf16[128,48,256]{2,1,0:T(8,128)(2,1)} async-done(((bf16[8,48,256]{2,1,0:T(8,128)(2,1)}), bf16[128,48,256]{2,1,0:T(8,128)(2,1)}) %all-gather.5.cloned.1.call-update) | async-done | bytes 3145744 | tf_op jit(solution)/shard_map/all_gather | solution.py:344
  70.0 3.4 %mlp.2 = bf16[128,2048]{1,0:T(8,128)(2,1)} custom-call(bf16[128,2048]{1,0:T(8,128)(2,1)S(1)} %bitcast.29, bf16[2,8,8,1,48,256]{5,4,3,2,1,0:T(8,128)(2,1)} %bitcast.47), custom_call_target="tpu_custom_call" | custom-call | flops 400000000 | bytes 4200000 | tf_op jit(solution)/shard_map/mlp/pallas_call | solution.py:261
  73.4 6.6 %all-to-all-start.2 = ((bf16[16,8,2048]{2,1,0:T(8,128)(2,1)}), bf16[16,8,2048]{2,1,0:T(8,128)(2,1)S(1)}, u32[]{:S(2)}, u32[]{:S(2)}) async-start(bf16[16,8,2048]{2,1,0:T(8,128)(2,1)} %bitcast.13), calls=%async_computation.2 | async-start | bytes 1048576 | tf_op jit(solution)/shard_map/all_to_all | solution.py:393
  80.1 9.6 %all-to-all-done.2 = bf16[16,8,2048]{2,1,0:T(8,128)(2,1)S(1)} async-done(((bf16[16,8,2048]{2,1,0:T(8,128)(2,1)}), bf16[16,8,2048]{2,1,0:T(8,128)(2,1)S(1)}, u32[]{:S(2)}, u32[]{:S(2)}) %all-to-all-start.2) | async-done | bytes 524320 | tf_op jit(solution)/shard_map/all_to_all | solution.py:393
  89.8 0.4 collective-permute-start.8
  90.2 2.6 %collective-permute-start.9 = (bf16[8,2048]{1,0:T(8,128)(2,1)S(1)}, bf16[8,2048]{1,0:T(8,128)(2,1)S(1)}, u32[]{:S(2)}, u32[]{:S(2)}) collective-permute-start(bf16[8,2048]{1,0:T(8,128)(2,1)S(1)} %fusion.8.refs_0_), channel_id=1, source_target_pairs={{0,128},{64,192},{128,0},{192,64},{1,129},{65,193},{129,1},{193,65... | collective-permute-start | bytes 98312 | tf_op jit(solution)/shard_map/ppermute | solution.py:305
  92.8 1.1 collective-permute-start.10
  93.9 2.7 %collective-permute-done.10.refs_3_ = bf16[8,2048]{1,0:T(8,128)(2,1)S(1)} collective-permute-done((bf16[8,2048]{1,0:T(8,128)(2,1)S(1)}, bf16[8,2048]{1,0:T(8,128)(2,1)S(1)}, u32[]{:S(2)}, u32[]{:S(2)}) %collective-permute-start.10) | collective-permute-done | bytes 32800 | tf_op jit(solution)/shard_map/ppermute | solution.py:305
  96.6 9.0 %attend.3 = (bf16[8,2048]{1,0:T(8,128)(2,1)S(1)}, bf16[8,2048]{1,0:T(8,128)(2,1)S(1)}, bf16[8,2048]{1,0:T(8,128)(2,1)S(1)}, bf16[8,2048]{1,0:T(8,128)(2,1)S(1)},...) custom-call(s32[8]{0:T(128)S(1)} %copy-done.6, s32[1]{0:T(128)} %bitcast.me, ...), custom_call_target="tpu_custom_call" | custom-call | flops 400000000 | bytes 13500000 | tf_op jit(solution)/shard_map/attend/pallas_call | solution.py:187
  105.6 1.2 collective-permute-start.12
  106.9 0.4 collective-permute-start.13
  107.6 1.3 collective-permute-done.12
  108.9 1.7 %collective-permute-done.13 = bf16[8,2048]{1,0:T(8,128)(2,1)S(1)} collective-permute-done((bf16[8,2048]{1,0:T(8,128)(2,1)S(1)}, bf16[8,2048]{1,0:T(8,128)(2,1)S(1)}, u32[]{:S(2)}, u32[]{:S(2)}) %collective-permute-start.13) | collective-permute-done | bytes 32800 | tf_op jit(solution)/shard_map/ppermute | solution.py:305
  110.9 8.6 %all_to_all.31 = bf16[8,8,2048]{2,1,0:T(8,128)(2,1)S(1)} all-to-all(bf16[8,8,2048]{2,1,0:T(8,128)(2,1)S(1)} %broadcast_in_dim.20), channel_id=1, replica_groups=mesh['section'=2,'tensor'=2,'z'=8,'y'=4,'xh'=2] {'tensor','y'}, dimensions={0} | all-to-all | bytes 524288 | tf_op jit(solution)/shard_map/all_to_all | solution.py:388
  119.4 4.8 %mlp.3 = bf16[2,4,2,8,1024]{4,3,2,1,0:T(8,128)(2,1)} custom-call(bf16[64,2048]{1,0:T(8,128)(2,1)S(1)} %bitcast.30, bf16[2,8,8,2,48,256]{5,4,3,2,1,0:T(8,128)(2,1)} %bitcast.46), custom_call_target="tpu_custom_call" | custom-call | flops 400000000 | bytes 4200000 | tf_op jit(solution)/shard_map/mlp/pallas_call | solution.py:261
  124.2 4.1 %all-to-all-start.5 = ((bf16[8,2,8,1024]{3,2,1,0:T(8,128)(2,1)}), bf16[8,2,8,1024]{3,2,1,0:T(8,128)(2,1)S(1)}, u32[]{:S(2)}, u32[]{:S(2)}) async-start(bf16[8,2,8,1024]{3,2,1,0:T(8,128)(2,1)} %bitcast.21), calls=%async_computation.5 | async-start | bytes 524288 | tf_op jit(solution)/shard_map/all_to_all | solution.py:403
  128.3 1.5 %collective-permute-start.14 = (bf16[8,1024]{1,0:T(8,128)(2,1)S(1)}, bf16[8,1024]{1,0:T(8,128)(2,1)S(1)}, u32[]{:S(2)}, u32[]{:S(2)}) collective-permute-start(bf16[8,1024]{1,0:T(8,128)(2,1)S(1)} %get-tuple-element.44), channel_id=1, source_target_pairs={{0,64},{64,0},{1,65},{65,1},{2,66},{66,2},{3,67},{67,3},{4,68},{68... | collective-permute-start | bytes 49160 | tf_op jit(solution)/shard_map/ppermute | solution.py:401
  129.9 4.6 %all-to-all-done.5 = bf16[8,2,8,1024]{3,2,1,0:T(8,128)(2,1)S(1)} async-done(((bf16[8,2,8,1024]{3,2,1,0:T(8,128)(2,1)}), bf16[8,2,8,1024]{3,2,1,0:T(8,128)(2,1)S(1)}, u32[]{:S(2)}, u32[]{:S(2)}) %all-to-all-start.5) | async-done | bytes 262176 | tf_op jit(solution)/shard_map/all_to_all | solution.py:403
  134.5 1.3 collective-permute-start.15
  135.8 3.0 %collective-permute-done.15 = bf16[2,8,1024]{2,1,0:T(8,128)(2,1)S(1)} collective-permute-done((bf16[2,8,1024]{2,1,0:T(8,128)(2,1)S(1)}, bf16[2,8,1024]{2,1,0:T(8,128)(2,1)S(1)}, u32[]{:S(2)}, u32[]{:S(2)}) %collective-permute-start.15) | collective-permute-done | bytes 32800 | tf_op jit(solution)/shard_map/ppermute | solution.py:406
  138.8 0.7 copy.16
  (52 shorter events, 1.6 us)
Async XLA Ops:
  6.5 0.9 copy-start
  7.4 0.9 copy-start.1
  8.3 0.9 copy-start.2
  9.3 4.4 %collective-permute-start.7 = (bf16[8,48,256]{2,1,0:T(8,128)(2,1)S(1)}, bf16[8,48,256]{2,1,0:T(8,128)(2,1)S(1)}, u32[]{:S(2)}, u32[]{:S(2)}) collective-permute-start(bf16[8,48,256]{2,1,0:T(8,128)(2,1)S(1)} %get-tuple-element.27), channel_id=1, source_target_pairs={{0,128},{128,0},{1,129},{129,1},{2,130},{130,2},{3,131},{131,3},{4... | collective-permute-start | bytes 589832 | tf_op jit(solution)/shard_map/ppermute | solution.py:333
  14.3 12.3 %all-to-all-start.1 = ((bf16[8,48,256]{2,1,0:T(8,128)(2,1)}), bf16[8,48,256]{2,1,0:T(8,128)(2,1)S(1)}, u32[]{:S(2)}, u32[]{:S(2)}) async-start(bf16[8,48,256]{2,1,0:T(8,128)(2,1)} %get-tuple-element.42), calls=%async_computation.1 | async-start | bytes 393216 | tf_op jit(solution)/shard_map/all_to_all | solution.py:336
  19.3 50.7 %all-gather.5.cloned.1.call-start = ((), (), s32[]{:S(2)}) async-start(), calls=%async_computation.6 | async-start | bytes 3342336 | tf_op jit(solution)/shard_map/all_gather | solution.py:344
  20.1 3.9 %collective-permute-start = (bf16[4,8,512]{2,1,0:T(8,128)(2,1)S(1)}, bf16[4,8,512]{2,1,0:T(8,128)(2,1)S(1)}, u32[]{:S(2)}, u32[]{:S(2)}) collective-permute-start(bf16[4,8,512]{2,1,0:T(8,128)(2,1)S(1)} %bitcast.31), channel_id=1, source_target_pairs={{0,64},{64,0},{128,192},{192,128},{1,65},{65,1},{129,193},{193,129... | collective-permute-start | bytes 98312 | tf_op jit(solution)/shard_map/ppermute | solution.py:305
  20.5 3.5 %collective-permute-start.1 = (bf16[4,8,512]{2,1,0:T(8,128)(2,1)S(1)}, bf16[4,8,512]{2,1,0:T(8,128)(2,1)S(1)}, u32[]{:S(2)}, u32[]{:S(2)}) collective-permute-start(bf16[4,8,512]{2,1,0:T(8,128)(2,1)S(1)} %bitcast.32), channel_id=1, source_target_pairs={{0,128},{64,192},{128,0},{192,64},{1,129},{65,193},{129,1},{193,65... | collective-permute-start | bytes 98312 | tf_op jit(solution)/shard_map/ppermute | solution.py:305
  21.4 3.6 %collective-permute-start.2 = (bf16[4,8,512]{2,1,0:T(8,128)(2,1)S(1)}, bf16[4,8,512]{2,1,0:T(8,128)(2,1)S(1)}, u32[]{:S(2)}, u32[]{:S(2)}) collective-permute-start(bf16[4,8,512]{2,1,0:T(8,128)(2,1)S(1)} %bitcast.33), channel_id=1, source_target_pairs={{0,192},{64,128},{128,64},{192,0},{1,193},{65,129},{129,65},{193,1... | collective-permute-start | bytes 98312 | tf_op jit(solution)/shard_map/ppermute | solution.py:305
  22.5 1.5 %collective-permute-start.6 = (f32[1,2048]{1,0:T(1,128)}, f32[1,2048]{1,0:T(1,128)S(1)}, u32[]{:S(2)}, u32[]{:S(2)}) collective-permute-start(f32[1,2048]{1,0:T(1,128)} %param.20), channel_id=1, source_target_pairs={{0,128},{128,0},{1,129},{129,1},{2,130},{130,2},{3,131},{131,3},{4... | collective-permute-start | bytes 24584 | tf_op jit(solution)/shard_map/ppermute | solution.py:338
  26.6 0.7 copy-start.8
  29.0 20.7 %all-to-all-start.4 = ((bf16[8,2,48,256]{3,2,1,0:T(8,128)(2,1)}), bf16[8,2,48,256]{3,2,1,0:T(8,128)(2,1)S(1)}, u32[]{:S(2)}, u32[]{:S(2)}) async-start(bf16[8,2,48,256]{3,2,1,0:T(8,128)(2,1)} %bitcast.19), calls=%async_computation.4 | async-start | bytes 786432 | tf_op jit(solution)/shard_map/all_to_all | solution.py:351
  34.6 84.8 %all-gather.7.cloned.1.call-start = ((), (), s32[]{:S(2)}) async-start(), calls=%async_computation.7 | async-start | bytes 6684672 | tf_op jit(solution)/shard_map/all_gather | solution.py:344
  34.8 0.7 copy-start.3
  35.5 0.7 copy-start.5
  36.2 14.4 %copy-start.9 = (f32[1,2048]{1,0:T(1,128)S(1)}, f32[1,2048]{1,0:T(1,128)}, u32[]{:S(2)}) copy-start(f32[1,2048]{1,0:T(1,128)} %param.20) | copy-start | bytes 24580
  45.1 35.0 %copy-start.10 = (s32[8]{0:T(128)S(1)}, s32[8]{0:T(128)}, u32[]{:S(2)}) copy-start(s32[8]{0:T(128)} %param.13) | copy-start | bytes 100
  45.1 51.5 %copy-start.4 = (f32[1,2048]{1,0:T(1,128)S(1)}, f32[1,2048]{1,0:T(1,128)}, u32[]{:S(2)}) copy-start(f32[1,2048]{1,0:T(1,128)} %refs_4_.3) | copy-start | bytes 24580
  45.1 51.5 %copy-start.6 = (s32[8]{0:T(128)S(1)}, s32[8]{0:T(128)}, u32[]{:S(2)}) copy-start(s32[8]{0:T(128)} %lens.3) | copy-start | bytes 100
  45.1 3.3 %collective-permute-start.4 = (bf16[8,2048]{1,0:T(8,128)(2,1)S(1)}, bf16[8,2048]{1,0:T(8,128)(2,1)S(1)}, u32[]{:S(2)}, u32[]{:S(2)}) collective-permute-start(bf16[8,2048]{1,0:T(8,128)(2,1)S(1)} %get-tuple-element.24), channel_id=1, source_target_pairs={{0,64},{64,0},{128,192},{192,128},{1,65},{65,1},{129,193},{193,129... | collective-permute-start | bytes 98312 | tf_op jit(solution)/shard_map/ppermute | solution.py:305
  45.2 4.3 %collective-permute-start.5 = (bf16[8,2048]{1,0:T(8,128)(2,1)S(1)}, bf16[8,2048]{1,0:T(8,128)(2,1)S(1)}, u32[]{:S(2)}, u32[]{:S(2)}) collective-permute-start(bf16[8,2048]{1,0:T(8,128)(2,1)S(1)} %get-tuple-element.25), channel_id=1, source_target_pairs={{0,192},{64,128},{128,64},{192,0},{1,193},{65,129},{129,65},{193,1... | collective-permute-start | bytes 98312 | tf_op jit(solution)/shard_map/ppermute | solution.py:305
  47.1 2.4 %collective-permute-start.3 = (bf16[8,2048]{1,0:T(8,128)(2,1)S(1)}, bf16[8,2048]{1,0:T(8,128)(2,1)S(1)}, u32[]{:S(2)}, u32[]{:S(2)}) collective-permute-start(bf16[8,2048]{1,0:T(8,128)(2,1)S(1)} %get-tuple-element.23), channel_id=1, source_target_pairs={{0,128},{64,192},{128,0},{192,64},{1,129},{65,193},{129,1},{193,65... | collective-permute-start | bytes 98312 | tf_op jit(solution)/shard_map/ppermute | solution.py:305
  49.7 0.8 copy-start.7
  73.4 16.3 %all-to-all-start.2 = ((bf16[16,8,2048]{2,1,0:T(8,128)(2,1)}), bf16[16,8,2048]{2,1,0:T(8,128)(2,1)S(1)}, u32[]{:S(2)}, u32[]{:S(2)}) async-start(bf16[16,8,2048]{2,1,0:T(8,128)(2,1)} %bitcast.13), calls=%async_computation.2 | async-start | bytes 1048576 | tf_op jit(solution)/shard_map/all_to_all | solution.py:393
  89.8 4.1 %collective-permute-start.8 = (bf16[8,2048]{1,0:T(8,128)(2,1)S(1)}, bf16[8,2048]{1,0:T(8,128)(2,1)S(1)}, u32[]{:S(2)}, u32[]{:S(2)}) collective-permute-start(bf16[8,2048]{1,0:T(8,128)(2,1)S(1)} %fusion.8.refs_0_), channel_id=1, source_target_pairs={{0,64},{64,0},{128,192},{192,128},{1,65},{65,1},{129,193},{193,129... | collective-permute-start | bytes 98312 | tf_op jit(solution)/shard_map/ppermute | solution.py:305
  90.2 3.7 %collective-permute-start.9 = (bf16[8,2048]{1,0:T(8,128)(2,1)S(1)}, bf16[8,2048]{1,0:T(8,128)(2,1)S(1)}, u32[]{:S(2)}, u32[]{:S(2)}) collective-permute-start(bf16[8,2048]{1,0:T(8,128)(2,1)S(1)} %fusion.8.refs_0_), channel_id=1, source_target_pairs={{0,128},{64,192},{128,0},{192,64},{1,129},{65,193},{129,1},{193,65... | collective-permute-start | bytes 98312 | tf_op jit(solution)/shard_map/ppermute | solution.py:305
  92.8 3.8 %collective-permute-start.10 = (bf16[8,2048]{1,0:T(8,128)(2,1)S(1)}, bf16[8,2048]{1,0:T(8,128)(2,1)S(1)}, u32[]{:S(2)}, u32[]{:S(2)}) collective-permute-start(bf16[8,2048]{1,0:T(8,128)(2,1)S(1)} %fusion.8.refs_0_), channel_id=1, source_target_pairs={{0,192},{64,128},{128,64},{192,0},{1,193},{65,129},{129,65},{193,1... | collective-permute-start | bytes 98312 | tf_op jit(solution)/shard_map/ppermute | solution.py:305
  105.6 3.3 %collective-permute-start.12 = (bf16[8,2048]{1,0:T(8,128)(2,1)S(1)}, bf16[8,2048]{1,0:T(8,128)(2,1)S(1)}, u32[]{:S(2)}, u32[]{:S(2)}) collective-permute-start(bf16[8,2048]{1,0:T(8,128)(2,1)S(1)} %get-tuple-element.33), channel_id=1, source_target_pairs={{0,64},{64,0},{128,192},{192,128},{1,65},{65,1},{129,193},{193,129... | collective-permute-start | bytes 98312 | tf_op jit(solution)/shard_map/ppermute | solution.py:305
  106.9 3.7 %collective-permute-start.13 = (bf16[8,2048]{1,0:T(8,128)(2,1)S(1)}, bf16[8,2048]{1,0:T(8,128)(2,1)S(1)}, u32[]{:S(2)}, u32[]{:S(2)}) collective-permute-start(bf16[8,2048]{1,0:T(8,128)(2,1)S(1)} %get-tuple-element.34), channel_id=1, source_target_pairs={{0,192},{64,128},{128,64},{192,0},{1,193},{65,129},{129,65},{193,1... | collective-permute-start | bytes 98312 | tf_op jit(solution)/shard_map/ppermute | solution.py:305
  107.3 3.3 %collective-permute-start.11 = (bf16[8,2048]{1,0:T(8,128)(2,1)S(1)}, bf16[8,2048]{1,0:T(8,128)(2,1)S(1)}, u32[]{:S(2)}, u32[]{:S(2)}) collective-permute-start(bf16[8,2048]{1,0:T(8,128)(2,1)S(1)} %get-tuple-element.32), channel_id=1, source_target_pairs={{0,128},{64,192},{128,0},{192,64},{1,129},{65,193},{129,1},{193,65... | collective-permute-start | bytes 98312 | tf_op jit(solution)/shard_map/ppermute | solution.py:305
  124.2 10.2 %all-to-all-start.5 = ((bf16[8,2,8,1024]{3,2,1,0:T(8,128)(2,1)}), bf16[8,2,8,1024]{3,2,1,0:T(8,128)(2,1)S(1)}, u32[]{:S(2)}, u32[]{:S(2)}) async-start(bf16[8,2,8,1024]{3,2,1,0:T(8,128)(2,1)} %bitcast.21), calls=%async_computation.5 | async-start | bytes 524288 | tf_op jit(solution)/shard_map/all_to_all | solution.py:403
  128.3 6.2 %collective-permute-start.14 = (bf16[8,1024]{1,0:T(8,128)(2,1)S(1)}, bf16[8,1024]{1,0:T(8,128)(2,1)S(1)}, u32[]{:S(2)}, u32[]{:S(2)}) collective-permute-start(bf16[8,1024]{1,0:T(8,128)(2,1)S(1)} %get-tuple-element.44), channel_id=1, source_target_pairs={{0,64},{64,0},{1,65},{65,1},{2,66},{66,2},{3,67},{67,3},{4,68},{68... | collective-permute-start | bytes 49160 | tf_op jit(solution)/shard_map/ppermute | solution.py:401
  134.5 4.3 %collective-permute-start.15 = (bf16[2,8,1024]{2,1,0:T(8,128)(2,1)S(1)}, bf16[2,8,1024]{2,1,0:T(8,128)(2,1)S(1)}, u32[]{:S(2)}, u32[]{:S(2)}) collective-permute-start(bf16[2,8,1024]{2,1,0:T(8,128)(2,1)S(1)} %add_convert_fusion), channel_id=1, source_target_pairs={{0,128},{1,129},{2,130},{3,131},{4,132},{5,133},{6,134},{7,135},{8... | collective-permute-start | bytes 98312 | tf_op jit(solution)/shard_map/ppermute | solution.py:406
Sparse Core Ops, SparseCore 0:
  27.4 42.5 all-gather.4
  71.8 44.5 all-gather.6

commit v2 on v1

--- a/solution.py
+++ b/solution.py
@@ -276,7 +276,15 @@
     )(tokens, gathered)
 
 
-def halves_kernel(section, gate, up, down, keep, give):
+def halves_kernel(section, gate_h, up_h, down_h, keep, give, gate, up, down, sems):
+    copies = [
+        pltpu.make_async_copy(h, v, sems.at[n])
+        for n, (h, v) in enumerate(((gate_h, gate), (up_h, up), (down_h, down)))
+    ]
+    for c in copies:
+        c.start()
+    for c in copies:
+        c.wait()
     for out, which in ((keep, section[0]), (give, 1 - section[0])):
         at = pl.ds(pl.multiple_of(which * 16, 16), 16)
         for g, w in enumerate((gate, up, down)):
@@ -289,9 +297,11 @@
     return pl.pallas_call(
         halves_kernel,
         out_shape=[jax.ShapeDtypeStruct((8, 48, FFS), jnp.bfloat16)] * 2,
-        in_specs=[pl.BlockSpec(memory_space=pltpu.SMEM), vmem, vmem, vmem],
+        in_specs=[pl.BlockSpec(memory_space=pltpu.SMEM)]
+        + [pl.BlockSpec(memory_space=pltpu.HBM)] * 3,
         out_specs=[vmem, vmem],
-        compiler_params=pltpu.CompilerParams(vmem_limit_bytes=VMEM_LIMIT),
+        scratch_shapes=[pltpu.VMEM((32, D), jnp.bfloat16)] * 3 + [pltpu.SemaphoreType.DMA((3,))],
+        compiler_params=pltpu.CompilerParams(vmem_limit_bytes=60 * 1024 * 1024),
         name="halves",
     )(section, gate, up, down)
 

time: 147 us -> 147 us (level)
  local copies, waits for them, and re-layouts: 7.91 us -> 5.2 us
  Pallas kernels: 26.2 us -> 28 us
    unnamed x23 -> x17, local copies, waits for them, and re-layouts: 6.29 us -> 3.59 us
    pallas_call x1, Pallas kernels: 0.03 us -> 1.82 us  [laid_halves(): pl.pallas_call(halves_kernel, out_shape=[jax.ShapeDtypeStruct((8, 48, FFS...]
where the time goes in v2:
time: 147 us
  starting transfers between devices  38.4 us (26%)
  waiting for transfers between devices  33.1 us (23%)
  Pallas kernels  28 us (19%)
  blocking collectives  25 us (17%)
  between operations  13.6 us (9%)
  local copies, waits for them, and re-layouts  5.2 us (4%)
  other arithmetic  3.23 us (2%)
    all_to_all x2, blocking collectives, local(): lax.all_to_all(jnp.broadcast_to(mlp_in[None], (group, ROWS, D)), axes, 0,...  25 us
    pallas_call x2, Pallas kernels, attend(): pl.pallas_call(functools.partial(attend_kernel, by_token), out_shape=[qua...  17.9 us
    ppermute x12, starting transfers between devices, exchanged(): lax.ppermute(blocks[k], CHIP, [(i, i ^ k) for i in range(4)])  10.4 us
    all_to_all x1, waiting for transfers between devices, local(): lax.all_to_all(share.reshape(group, ROWS, D), axes, 0, 0, tiled=True)  9.59 us
    ppermute x12, waiting for transfers between devices, exchanged(): lax.ppermute(blocks[k], CHIP, [(i, i ^ k) for i in range(4)])  9.21 us
    pallas_call x2, Pallas kernels, mlp(): pl.pallas_call(functools.partial(mlp_kernel, halves), out_shape=jax.Shape...  8.21 us
    all_to_all x1, starting transfers between devices, local(): lax.all_to_all(share.reshape(group, ROWS, D), axes, 0, 0, tiled=True)  6.59 us
    all_to_all x1, starting transfers between devices, local(): lax.all_to_all(after(pieces[3], slices), ('y', 'xh'), 0, 0, tiled=True)  5.66 us
  transfers between devices with their start and end apart: 22, of which 13 were waited for; matrix products, arithmetic and copies ran while one was open for 2% of the time, Pallas kernels for 15%

profile of v2, /device:TPU:1, one launch (start us, length us, event | category | flops | bytes accessed | tf_op | source)
XLA Modules:
  0.0 146.5 jit_solution(18159311978045583330)
XLA Ops:
  6.5 1.8 %halves.1 = (bf16[8,48,256]{2,1,0:T(8,128)(2,1)}, bf16[8,48,256]{2,1,0:T(8,128)(2,1)}) custom-call(s32[1]{0:T(128)} %bitcast.8.section, bf16[32,2048]{1,0:T(8,128)(2,1)} %bitcast.46, bf16[32,2048]{1,0:T(8,128)(2,1)} %bitcast.47, bf16[32,2048]{1,0:T(8,128)(2,1)} %bitcast.48), custom_call_target="tpu_custom_call" | custom-call | tf_op jit(solution)/shard_map/halves/pallas_call | solution.py:297
  8.4 3.3 %collective-permute-start.7 = (bf16[8,48,256]{2,1,0:T(8,128)(2,1)}, bf16[8,48,256]{2,1,0:T(8,128)(2,1)S(1)}, u32[]{:S(2)}, u32[]{:S(2)}) collective-permute-start(bf16[8,48,256]{2,1,0:T(8,128)(2,1)} %get-tuple-element.27), channel_id=1, source_target_pairs={{0,128},{128,0},{1,129},{129,1},{2,130},{130,2},{3,131},{131,3},{4... | collective-permute-start | bytes 589832 | tf_op jit(solution)/shard_map/ppermute | solution.py:343
  11.7 1.3 collective-permute-done.7
  12.9 1.6 %broadcast_select_fusion = (bf16[8,48,256]{2,1,0:T(8,128)(2,1)S(1)}, bf16[8,48,256]{2,1,0:T(8,128)(2,1)}) fusion(bf16[8,48,256]{2,1,0:T(8,128)(2,1)} %get-tuple-element.26, bf16[8,48,256]{2,1,0:T(8,128)(2,1)S(1)} %collective-permute-done.7, pred[]{:T(512)S(6)} %eq.8, pred[]{:T(512)S(6)} %eq.6), kind=kLoop, calls=%fused_computation.2 | loop fusion | flops 196608 | bytes 786434 | tf_op jit(solution)/shard_map/jit(_where)/select_n | solution.py:345
  14.6 4.9 %all-to-all-start.1 = ((bf16[8,48,256]{2,1,0:T(8,128)(2,1)}), bf16[8,48,256]{2,1,0:T(8,128)(2,1)S(1)}, u32[]{:S(2)}, u32[]{:S(2)}) async-start(bf16[8,48,256]{2,1,0:T(8,128)(2,1)} %get-tuple-element.42), calls=%async_computation.1 | async-start | bytes 393216 | tf_op jit(solution)/shard_map/all_to_all | solution.py:346
  19.5 0.8 copy.18
  20.3 0.4 collective-permute-start
  20.7 0.9 collective-permute-start.1
  21.6 1.0 collective-permute-start.2
  22.7 0.5 collective-permute-start.6
  23.2 1.0 collective-permute-done.6
  24.2 1.0 collective-permute-done.2.refs_3_
  25.3 1.5 %all-to-all-done.1 = bf16[8,48,256]{2,1,0:T(8,128)(2,1)S(1)} async-done(((bf16[8,48,256]{2,1,0:T(8,128)(2,1)}), bf16[8,48,256]{2,1,0:T(8,128)(2,1)S(1)}, u32[]{:S(2)}, u32[]{:S(2)}) %all-to-all-start.1) | async-done | bytes 196640 | tf_op jit(solution)/shard_map/all_to_all | solution.py:346
  26.8 0.7 copy-done.5
  27.5 0.7 add_convert_fusion.3
  28.3 0.1 fusion.9
  28.4 0.8 broadcast_in_dim.22
  29.2 5.7 %all-to-all-start.4 = ((bf16[8,2,48,256]{3,2,1,0:T(8,128)(2,1)}), bf16[8,2,48,256]{3,2,1,0:T(8,128)(2,1)S(1)}, u32[]{:S(2)}, u32[]{:S(2)}) async-start(bf16[8,2,48,256]{3,2,1,0:T(8,128)(2,1)} %bitcast.19), calls=%async_computation.4 | async-start | bytes 786432 | tf_op jit(solution)/shard_map/all_to_all | solution.py:361
  35.0 0.7 copy-done
  35.7 0.7 copy-done.2
  36.4 8.9 %attend.2 = (bf16[8,2048]{1,0:T(8,128)(2,1)S(1)}, bf16[8,2048]{1,0:T(8,128)(2,1)S(1)}, bf16[8,2048]{1,0:T(8,128)(2,1)S(1)}, bf16[8,2048]{1,0:T(8,128)(2,1)S(1)},...) custom-call(s32[8]{0:T(128)S(1)} %copy-done.2, s32[1]{0:T(128)} %bitcast.me, bf16[4,8,512]{2,1,0:T(8,128)(2,1)S(1)} %bitcast.34, ...), custom_call_target="tpu_custom_call" | custom-call | flops 400000000 | bytes 13500000 | tf_op jit(solution)/shard_map/attend/pallas_call | solution.py:187
  45.4 1.9 %collective-permute-start.5 = (bf16[8,2048]{1,0:T(8,128)(2,1)S(1)}, bf16[8,2048]{1,0:T(8,128)(2,1)S(1)}, u32[]{:S(2)}, u32[]{:S(2)}) collective-permute-start(bf16[8,2048]{1,0:T(8,128)(2,1)S(1)} %get-tuple-element.25), channel_id=1, source_target_pairs={{0,192},{64,128},{128,64},{192,0},{1,193},{65,129},{129,65},{193,1... | collective-permute-start | bytes 98312 | tf_op jit(solution)/shard_map/ppermute | solution.py:315
  47.3 1.3 collective-permute-done.4
  48.6 1.2 collective-permute-done.5
  49.9 0.8 copy-done.4
  50.9 16.4 %all_to_all.30 = bf16[16,8,2048]{2,1,0:T(8,128)(2,1)S(1)} all-to-all(bf16[16,8,2048]{2,1,0:T(8,128)(2,1)S(1)} %broadcast_in_dim.19), channel_id=1, replica_groups=mesh['section'=2,'tensor'=2,'z'=8,'y'=4,'xh'=2] {'tensor','y','xh'}, dimensions={0} | all-to-all | bytes 1048576 | tf_op jit(solution)/shard_map/all_to_all | solution.py:398
  67.3 2.9 %all-gather.5.cloned.1.call-done = bf16[128,48,256]{2,1,0:T(8,128)(2,1)} async-done(((bf16[8,48,256]{2,1,0:T(8,128)(2,1)}), bf16[128,48,256]{2,1,0:T(8,128)(2,1)}) %all-gather.5.cloned.1.call-update) | async-done | bytes 3145744 | tf_op jit(solution)/shard_map/all_gather | solution.py:354
  70.2 3.4 %mlp.2 = bf16[128,2048]{1,0:T(8,128)(2,1)} custom-call(bf16[128,2048]{1,0:T(8,128)(2,1)S(1)} %bitcast.29, bf16[2,8,8,1,48,256]{5,4,3,2,1,0:T(8,128)(2,1)} %bitcast.44), custom_call_target="tpu_custom_call" | custom-call | flops 400000000 | bytes 4200000 | tf_op jit(solution)/shard_map/mlp/pallas_call | solution.py:261
  73.6 6.6 %all-to-all-start.2 = ((bf16[16,8,2048]{2,1,0:T(8,128)(2,1)}), bf16[16,8,2048]{2,1,0:T(8,128)(2,1)S(1)}, u32[]{:S(2)}, u32[]{:S(2)}) async-start(bf16[16,8,2048]{2,1,0:T(8,128)(2,1)} %bitcast.13), calls=%async_computation.2 | async-start | bytes 1048576 | tf_op jit(solution)/shard_map/all_to_all | solution.py:403
  80.3 9.6 %all-to-all-done.2 = bf16[16,8,2048]{2,1,0:T(8,128)(2,1)S(1)} async-done(((bf16[16,8,2048]{2,1,0:T(8,128)(2,1)}), bf16[16,8,2048]{2,1,0:T(8,128)(2,1)S(1)}, u32[]{:S(2)}, u32[]{:S(2)}) %all-to-all-start.2) | async-done | bytes 524320 | tf_op jit(solution)/shard_map/all_to_all | solution.py:403
  90.0 0.4 collective-permute-start.8
  90.4 2.6 %collective-permute-start.9 = (bf16[8,2048]{1,0:T(8,128)(2,1)S(1)}, bf16[8,2048]{1,0:T(8,128)(2,1)S(1)}, u32[]{:S(2)}, u32[]{:S(2)}) collective-permute-start(bf16[8,2048]{1,0:T(8,128)(2,1)S(1)} %fusion.8.refs_0_), channel_id=1, source_target_pairs={{0,128},{64,192},{128,0},{192,64},{1,129},{65,193},{129,1},{193,65... | collective-permute-start | bytes 98312 | tf_op jit(solution)/shard_map/ppermute | solution.py:315
  93.0 1.1 collective-permute-start.10
  94.1 2.7 %collective-permute-done.10.refs_3_ = bf16[8,2048]{1,0:T(8,128)(2,1)S(1)} collective-permute-done((bf16[8,2048]{1,0:T(8,128)(2,1)S(1)}, bf16[8,2048]{1,0:T(8,128)(2,1)S(1)}, u32[]{:S(2)}, u32[]{:S(2)}) %collective-permute-start.10) | collective-permute-done | bytes 32800 | tf_op jit(solution)/shard_map/ppermute | solution.py:315
  96.8 9.0 %attend.3 = (bf16[8,2048]{1,0:T(8,128)(2,1)S(1)}, bf16[8,2048]{1,0:T(8,128)(2,1)S(1)}, bf16[8,2048]{1,0:T(8,128)(2,1)S(1)}, bf16[8,2048]{1,0:T(8,128)(2,1)S(1)},...) custom-call(s32[8]{0:T(128)S(1)} %copy-done.3, s32[1]{0:T(128)} %bitcast.me, ...), custom_call_target="tpu_custom_call" | custom-call | flops 400000000 | bytes 13500000 | tf_op jit(solution)/shard_map/attend/pallas_call | solution.py:187
  105.8 1.2 collective-permute-start.12
  107.1 0.4 collective-permute-start.13
  107.5 0.3 collective-permute-start.11
  107.8 1.3 collective-permute-done.12
  109.1 1.7 %collective-permute-done.13 = bf16[8,2048]{1,0:T(8,128)(2,1)S(1)} collective-permute-done((bf16[8,2048]{1,0:T(8,128)(2,1)S(1)}, bf16[8,2048]{1,0:T(8,128)(2,1)S(1)}, u32[]{:S(2)}, u32[]{:S(2)}) %collective-permute-start.13) | collective-permute-done | bytes 32800 | tf_op jit(solution)/shard_map/ppermute | solution.py:315
  111.1 8.6 %all_to_all.31 = bf16[8,8,2048]{2,1,0:T(8,128)(2,1)S(1)} all-to-all(bf16[8,8,2048]{2,1,0:T(8,128)(2,1)S(1)} %broadcast_in_dim.20), channel_id=1, replica_groups=mesh['section'=2,'tensor'=2,'z'=8,'y'=4,'xh'=2] {'tensor','y'}, dimensions={0} | all-to-all | bytes 524288 | tf_op jit(solution)/shard_map/all_to_all | solution.py:398
  119.6 4.8 %mlp.3 = bf16[2,4,2,8,1024]{4,3,2,1,0:T(8,128)(2,1)} custom-call(bf16[64,2048]{1,0:T(8,128)(2,1)S(1)} %bitcast.30, bf16[2,8,8,2,48,256]{5,4,3,2,1,0:T(8,128)(2,1)} %bitcast.43), custom_call_target="tpu_custom_call" | custom-call | flops 400000000 | bytes 4200000 | tf_op jit(solution)/shard_map/mlp/pallas_call | solution.py:261
  124.4 4.1 %all-to-all-start.5 = ((bf16[8,2,8,1024]{3,2,1,0:T(8,128)(2,1)}), bf16[8,2,8,1024]{3,2,1,0:T(8,128)(2,1)S(1)}, u32[]{:S(2)}, u32[]{:S(2)}) async-start(bf16[8,2,8,1024]{3,2,1,0:T(8,128)(2,1)} %bitcast.21), calls=%async_computation.5 | async-start | bytes 524288 | tf_op jit(solution)/shard_map/all_to_all | solution.py:413
  128.5 1.5 %collective-permute-start.14 = (bf16[8,1024]{1,0:T(8,128)(2,1)S(1)}, bf16[8,1024]{1,0:T(8,128)(2,1)S(1)}, u32[]{:S(2)}, u32[]{:S(2)}) collective-permute-start(bf16[8,1024]{1,0:T(8,128)(2,1)S(1)} %get-tuple-element.44), channel_id=1, source_target_pairs={{0,64},{64,0},{1,65},{65,1},{2,66},{66,2},{3,67},{67,3},{4,68},{68... | collective-permute-start | bytes 49160 | tf_op jit(solution)/shard_map/ppermute | solution.py:411
  130.1 4.6 %all-to-all-done.5 = bf16[8,2,8,1024]{3,2,1,0:T(8,128)(2,1)S(1)} async-done(((bf16[8,2,8,1024]{3,2,1,0:T(8,128)(2,1)}), bf16[8,2,8,1024]{3,2,1,0:T(8,128)(2,1)S(1)}, u32[]{:S(2)}, u32[]{:S(2)}) %all-to-all-start.5) | async-done | bytes 262176 | tf_op jit(solution)/shard_map/all_to_all | solution.py:413
  134.7 1.3 collective-permute-start.15
  136.0 3.0 %collective-permute-done.15 = bf16[2,8,1024]{2,1,0:T(8,128)(2,1)S(1)} collective-permute-done((bf16[2,8,1024]{2,1,0:T(8,128)(2,1)S(1)}, bf16[2,8,1024]{2,1,0:T(8,128)(2,1)S(1)}, u32[]{:S(2)}, u32[]{:S(2)}) %collective-permute-start.15) | collective-permute-done | bytes 32800 | tf_op jit(solution)/shard_map/ppermute | solution.py:416
  139.0 0.7 copy.16
  (46 shorter events, 1.2 us)
Async XLA Ops:
  8.4 4.6 %collective-permute-start.7 = (bf16[8,48,256]{2,1,0:T(8,128)(2,1)}, bf16[8,48,256]{2,1,0:T(8,128)(2,1)S(1)}, u32[]{:S(2)}, u32[]{:S(2)}) collective-permute-start(bf16[8,48,256]{2,1,0:T(8,128)(2,1)} %get-tuple-element.27), channel_id=1, source_target_pairs={{0,128},{128,0},{1,129},{129,1},{2,130},{130,2},{3,131},{131,3},{4... | collective-permute-start | bytes 589832 | tf_op jit(solution)/shard_map/ppermute | solution.py:343
  14.6 12.3 %all-to-all-start.1 = ((bf16[8,48,256]{2,1,0:T(8,128)(2,1)}), bf16[8,48,256]{2,1,0:T(8,128)(2,1)S(1)}, u32[]{:S(2)}, u32[]{:S(2)}) async-start(bf16[8,48,256]{2,1,0:T(8,128)(2,1)} %get-tuple-element.42), calls=%async_computation.1 | async-start | bytes 393216 | tf_op jit(solution)/shard_map/all_to_all | solution.py:346
  19.5 50.7 %all-gather.5.cloned.1.call-start = ((), (), s32[]{:S(2)}) async-start(), calls=%async_computation.6 | async-start | bytes 3342336 | tf_op jit(solution)/shard_map/all_gather | solution.py:354
  20.3 3.9 %collective-permute-start = (bf16[4,8,512]{2,1,0:T(8,128)(2,1)S(1)}, bf16[4,8,512]{2,1,0:T(8,128)(2,1)S(1)}, u32[]{:S(2)}, u32[]{:S(2)}) collective-permute-start(bf16[4,8,512]{2,1,0:T(8,128)(2,1)S(1)} %bitcast.31), channel_id=1, source_target_pairs={{0,64},{64,0},{128,192},{192,128},{1,65},{65,1},{129,193},{193,129... | collective-permute-start | bytes 98312 | tf_op jit(solution)/shard_map/ppermute | solution.py:315
  20.7 3.5 %collective-permute-start.1 = (bf16[4,8,512]{2,1,0:T(8,128)(2,1)S(1)}, bf16[4,8,512]{2,1,0:T(8,128)(2,1)S(1)}, u32[]{:S(2)}, u32[]{:S(2)}) collective-permute-start(bf16[4,8,512]{2,1,0:T(8,128)(2,1)S(1)} %bitcast.32), channel_id=1, source_target_pairs={{0,128},{64,192},{128,0},{192,64},{1,129},{65,193},{129,1},{193,65... | collective-permute-start | bytes 98312 | tf_op jit(solution)/shard_map/ppermute | solution.py:315
  21.6 3.6 %collective-permute-start.2 = (bf16[4,8,512]{2,1,0:T(8,128)(2,1)S(1)}, bf16[4,8,512]{2,1,0:T(8,128)(2,1)S(1)}, u32[]{:S(2)}, u32[]{:S(2)}) collective-permute-start(bf16[4,8,512]{2,1,0:T(8,128)(2,1)S(1)} %bitcast.33), channel_id=1, source_target_pairs={{0,192},{64,128},{128,64},{192,0},{1,193},{65,129},{129,65},{193,1... | collective-permute-start | bytes 98312 | tf_op jit(solution)/shard_map/ppermute | solution.py:315
  22.7 1.5 %collective-permute-start.6 = (f32[1,2048]{1,0:T(1,128)}, f32[1,2048]{1,0:T(1,128)S(1)}, u32[]{:S(2)}, u32[]{:S(2)}) collective-permute-start(f32[1,2048]{1,0:T(1,128)} %param.20), channel_id=1, source_target_pairs={{0,128},{128,0},{1,129},{129,1},{2,130},{130,2},{3,131},{131,3},{4... | collective-permute-start | bytes 24584 | tf_op jit(solution)/shard_map/ppermute | solution.py:348
  26.8 0.7 copy-start.5
  29.2 20.7 %all-to-all-start.4 = ((bf16[8,2,48,256]{3,2,1,0:T(8,128)(2,1)}), bf16[8,2,48,256]{3,2,1,0:T(8,128)(2,1)S(1)}, u32[]{:S(2)}, u32[]{:S(2)}) async-start(bf16[8,2,48,256]{3,2,1,0:T(8,128)(2,1)} %bitcast.19), calls=%async_computation.4 | async-start | bytes 786432 | tf_op jit(solution)/shard_map/all_to_all | solution.py:361
  34.9 84.8 %all-gather.7.cloned.1.call-start = ((), (), s32[]{:S(2)}) async-start(), calls=%async_computation.7 | async-start | bytes 6684672 | tf_op jit(solution)/shard_map/all_gather | solution.py:354
  35.0 0.7 copy-start
  35.7 0.7 copy-start.2
  36.4 14.3 %copy-start.6 = (f32[1,2048]{1,0:T(1,128)S(1)}, f32[1,2048]{1,0:T(1,128)}, u32[]{:S(2)}) copy-start(f32[1,2048]{1,0:T(1,128)} %param.20) | copy-start | bytes 24580
  45.3 34.9 %copy-start.7 = (s32[8]{0:T(128)S(1)}, s32[8]{0:T(128)}, u32[]{:S(2)}) copy-start(s32[8]{0:T(128)} %param.13) | copy-start | bytes 100
  45.3 51.5 %copy-start.1 = (f32[1,2048]{1,0:T(1,128)S(1)}, f32[1,2048]{1,0:T(1,128)}, u32[]{:S(2)}) copy-start(f32[1,2048]{1,0:T(1,128)} %refs_4_.3) | copy-start | bytes 24580
  45.3 51.5 %copy-start.3 = (s32[8]{0:T(128)S(1)}, s32[8]{0:T(128)}, u32[]{:S(2)}) copy-start(s32[8]{0:T(128)} %lens.3) | copy-start | bytes 100
  45.3 3.3 %collective-permute-start.4 = (bf16[8,2048]{1,0:T(8,128)(2,1)S(1)}, bf16[8,2048]{1,0:T(8,128)(2,1)S(1)}, u32[]{:S(2)}, u32[]{:S(2)}) collective-permute-start(bf16[8,2048]{1,0:T(8,128)(2,1)S(1)} %get-tuple-element.24), channel_id=1, source_target_pairs={{0,64},{64,0},{128,192},{192,128},{1,65},{65,1},{129,193},{193,129... | collective-permute-start | bytes 98312 | tf_op jit(solution)/shard_map/ppermute | solution.py:315
  45.4 4.3 %collective-permute-start.5 = (bf16[8,2048]{1,0:T(8,128)(2,1)S(1)}, bf16[8,2048]{1,0:T(8,128)(2,1)S(1)}, u32[]{:S(2)}, u32[]{:S(2)}) collective-permute-start(bf16[8,2048]{1,0:T(8,128)(2,1)S(1)} %get-tuple-element.25), channel_id=1, source_target_pairs={{0,192},{64,128},{128,64},{192,0},{1,193},{65,129},{129,65},{193,1... | collective-permute-start | bytes 98312 | tf_op jit(solution)/shard_map/ppermute | solution.py:315
  47.3 2.4 %collective-permute-start.3 = (bf16[8,2048]{1,0:T(8,128)(2,1)S(1)}, bf16[8,2048]{1,0:T(8,128)(2,1)S(1)}, u32[]{:S(2)}, u32[]{:S(2)}) collective-permute-start(bf16[8,2048]{1,0:T(8,128)(2,1)S(1)} %get-tuple-element.23), channel_id=1, source_target_pairs={{0,128},{64,192},{128,0},{192,64},{1,129},{65,193},{129,1},{193,65... | collective-permute-start | bytes 98312 | tf_op jit(solution)/shard_map/ppermute | solution.py:315
  49.9 0.8 copy-start.4
  73.6 16.2 %all-to-all-start.2 = ((bf16[16,8,2048]{2,1,0:T(8,128)(2,1)}), bf16[16,8,2048]{2,1,0:T(8,128)(2,1)S(1)}, u32[]{:S(2)}, u32[]{:S(2)}) async-start(bf16[16,8,2048]{2,1,0:T(8,128)(2,1)} %bitcast.13), calls=%async_computation.2 | async-start | bytes 1048576 | tf_op jit(solution)/shard_map/all_to_all | solution.py:403
  90.0 4.1 %collective-permute-start.8 = (bf16[8,2048]{1,0:T(8,128)(2,1)S(1)}, bf16[8,2048]{1,0:T(8,128)(2,1)S(1)}, u32[]{:S(2)}, u32[]{:S(2)}) collective-permute-start(bf16[8,2048]{1,0:T(8,128)(2,1)S(1)} %fusion.8.refs_0_), channel_id=1, source_target_pairs={{0,64},{64,0},{128,192},{192,128},{1,65},{65,1},{129,193},{193,129... | collective-permute-start | bytes 98312 | tf_op jit(solution)/shard_map/ppermute | solution.py:315
  90.4 3.7 %collective-permute-start.9 = (bf16[8,2048]{1,0:T(8,128)(2,1)S(1)}, bf16[8,2048]{1,0:T(8,128)(2,1)S(1)}, u32[]{:S(2)}, u32[]{:S(2)}) collective-permute-start(bf16[8,2048]{1,0:T(8,128)(2,1)S(1)} %fusion.8.refs_0_), channel_id=1, source_target_pairs={{0,128},{64,192},{128,0},{192,64},{1,129},{65,193},{129,1},{193,65... | collective-permute-start | bytes 98312 | tf_op jit(solution)/shard_map/ppermute | solution.py:315
  93.0 3.8 %collective-permute-start.10 = (bf16[8,2048]{1,0:T(8,128)(2,1)S(1)}, bf16[8,2048]{1,0:T(8,128)(2,1)S(1)}, u32[]{:S(2)}, u32[]{:S(2)}) collective-permute-start(bf16[8,2048]{1,0:T(8,128)(2,1)S(1)} %fusion.8.refs_0_), channel_id=1, source_target_pairs={{0,192},{64,128},{128,64},{192,0},{1,193},{65,129},{129,65},{193,1... | collective-permute-start | bytes 98312 | tf_op jit(solution)/shard_map/ppermute | solution.py:315
  105.8 3.3 %collective-permute-start.12 = (bf16[8,2048]{1,0:T(8,128)(2,1)S(1)}, bf16[8,2048]{1,0:T(8,128)(2,1)S(1)}, u32[]{:S(2)}, u32[]{:S(2)}) collective-permute-start(bf16[8,2048]{1,0:T(8,128)(2,1)S(1)} %get-tuple-element.33), channel_id=1, source_target_pairs={{0,64},{64,0},{128,192},{192,128},{1,65},{65,1},{129,193},{193,129... | collective-permute-start | bytes 98312 | tf_op jit(solution)/shard_map/ppermute | solution.py:315
  107.1 3.7 %collective-permute-start.13 = (bf16[8,2048]{1,0:T(8,128)(2,1)S(1)}, bf16[8,2048]{1,0:T(8,128)(2,1)S(1)}, u32[]{:S(2)}, u32[]{:S(2)}) collective-permute-start(bf16[8,2048]{1,0:T(8,128)(2,1)S(1)} %get-tuple-element.34), channel_id=1, source_target_pairs={{0,192},{64,128},{128,64},{192,0},{1,193},{65,129},{129,65},{193,1... | collective-permute-start | bytes 98312 | tf_op jit(solution)/shard_map/ppermute | solution.py:315
  107.5 3.3 %collective-permute-start.11 = (bf16[8,2048]{1,0:T(8,128)(2,1)S(1)}, bf16[8,2048]{1,0:T(8,128)(2,1)S(1)}, u32[]{:S(2)}, u32[]{:S(2)}) collective-permute-start(bf16[8,2048]{1,0:T(8,128)(2,1)S(1)} %get-tuple-element.32), channel_id=1, source_target_pairs={{0,128},{64,192},{128,0},{192,64},{1,129},{65,193},{129,1},{193,65... | collective-permute-start | bytes 98312 | tf_op jit(solution)/shard_map/ppermute | solution.py:315
  124.4 10.2 %all-to-all-start.5 = ((bf16[8,2,8,1024]{3,2,1,0:T(8,128)(2,1)}), bf16[8,2,8,1024]{3,2,1,0:T(8,128)(2,1)S(1)}, u32[]{:S(2)}, u32[]{:S(2)}) async-start(bf16[8,2,8,1024]{3,2,1,0:T(8,128)(2,1)} %bitcast.21), calls=%async_computation.5 | async-start | bytes 524288 | tf_op jit(solution)/shard_map/all_to_all | solution.py:413
  128.5 6.2 %collective-permute-start.14 = (bf16[8,1024]{1,0:T(8,128)(2,1)S(1)}, bf16[8,1024]{1,0:T(8,128)(2,1)S(1)}, u32[]{:S(2)}, u32[]{:S(2)}) collective-permute-start(bf16[8,1024]{1,0:T(8,128)(2,1)S(1)} %get-tuple-element.44), channel_id=1, source_target_pairs={{0,64},{64,0},{1,65},{65,1},{2,66},{66,2},{3,67},{67,3},{4,68},{68... | collective-permute-start | bytes 49160 | tf_op jit(solution)/shard_map/ppermute | solution.py:411
  134.7 4.3 %collective-permute-start.15 = (bf16[2,8,1024]{2,1,0:T(8,128)(2,1)S(1)}, bf16[2,8,1024]{2,1,0:T(8,128)(2,1)S(1)}, u32[]{:S(2)}, u32[]{:S(2)}) collective-permute-start(bf16[2,8,1024]{2,1,0:T(8,128)(2,1)S(1)} %add_convert_fusion), channel_id=1, source_target_pairs={{0,128},{1,129},{2,130},{3,131},{4,132},{5,133},{6,134},{7,135},{8... | collective-permute-start | bytes 98312 | tf_op jit(solution)/shard_map/ppermute | solution.py:416
Sparse Core Ops, SparseCore 0:
  27.7 42.5 all-gather.4
  72.0 44.5 all-gather.6
